TPU v7x, 32 devices: a whole 2x2x4 slice. The times are simulated.
32 devices in a mesh: tile: 4 (over x, core), chan: 4 (over z), beam: 2 (over y).
Axes of the slice: x: 2, y: 2, z: 4, core: 2. Of those that a mesh axis runs over, the one named last changes fastest.
Arguments:
- voltages: bfloat16 [32, 128, 2, 2, 1536], P(None, 'tile', None, None, 'chan'), may hold values from -6 to 6
- calib_gain: float32 [128, 2, 2, 1536], P(('tile', 'beam'), None, None, 'chan'), may hold values from -0.375 to 0.375
- tile_flags: int32 [128], P(('tile', 'beam')), may hold values 0 or 1
- delays: float32 [64, 128], P(None, 'tile'), may hold values from -4 to 4
- pointing: int32 [2], P('beam'), may hold values from 0 to 63
- synth_filter: float32 [12, 128], replicated, may hold values from -0.5 to 0.5
Outputs:
- streams: float32 [32, 2, 2, 12, 256], P('tile', 'beam', None, 'chan')
Inputs may be any that keep to these rules, and one draw needn't show every extreme that they name: `tile_flags`: 1 marks a tile in use. `pointing`: a row of delays, one of 64.
All inputs are finite; a program needn't handle non-finite values. No bound on the sum of `tile_flags` on one device may be relied on, other than what follows from the above.
Results may differ from a plain program's by a relative error of at most 0.0003.
Values sent between devices are 32-bit elements; how exact they have to be, the bound alone decides.
A program may use at most 64 MiB of HBM per device.

v0:
```python
import functools
import math

import jax
import jax.numpy as jnp
import numpy as np
from jax import lax
from jax.experimental import pallas as pl
from jax.experimental.pallas import tpu as pltpu
from jax.sharding import PartitionSpec as P

COARSE = 12
LANES = 128
MESH = pl.DeviceIdType.MESH
F32 = jnp.float32
BF16 = jnp.bfloat16


def even_fit(func, degree):
    series = np.polynomial.chebyshev.Chebyshev.interpolate(
        lambda u: func(np.sqrt(u)), degree, domain=[0.0, 0.25]
    )
    return [float(v) for v in series.convert(kind=np.polynomial.Polynomial).coef]


COS_COEF = even_fit(lambda r: np.cos(2 * np.pi * r), 7)
SIN_COEF = even_fit(lambda r: 2 * np.pi * np.sinc(2 * r), 7)


def horner(coef, u):
    total = jnp.full_like(u, coef[-1])
    for value in coef[-2::-1]:
        total = total * u + value
    return total


def split_bf16(table):
    high = table.astype(BF16)
    low = (table - high.astype(np.float64)).astype(BF16)
    return high, low


def dft_table(nz, fz):
    k = nz * fz
    f = np.arange(k)
    m = np.arange(k)
    angle = 2 * np.pi * (f[:, None] * m[None, :] % k) / k
    cosine, sine = np.cos(angle) / math.sqrt(k), np.sin(angle) / math.sqrt(k)
    out = np.zeros((nz, 2, 2, fz, 2, 2, k))
    for p in range(2):
        out[:, p, 0, :, p, 0] = cosine.reshape(nz, fz, k)
        out[:, p, 0, :, p, 1] = sine.reshape(nz, fz, k)
        out[:, p, 1, :, p, 0] = -sine.reshape(nz, fz, k)
        out[:, p, 1, :, p, 1] = cosine.reshape(nz, fz, k)
    return split_bf16(out.reshape(nz * 4 * fz, 4 * k))


def gather_table(nz, fz, cz):
    width = fz * COARSE
    out = np.zeros((width, width), np.float64)
    for c in range(cz):
        for z in range(nz):
            for f in range(fz):
                out[f * COARSE + z * cz + c, (c * nz + z) * fz + f] = 1.0
    return out.astype(BF16)


def kernel(
    cfg,
    volt_ref,
    gain_ref,
    flag_src,
    delay_src,
    point_src,
    synth_src,
    chan_src,
    perm_src,
    dfth_ref,
    dftl_ref,
    out_ref,
    flag_ref,
    delay_ref,
    point_ref,
    synth_ref,
    chan_ref,
    perm_ref,
    small_sem,
    volt,
    own_gain,
    gains,
    w_re,
    w_im,
    acc,
    part,
    recv,
    packed,
    inbox,
    spec,
    dft_h,
    dft_l,
    volt_sem,
    table_sem,
    own_sem,
    gain_send,
    gain_recv,
    part_send,
    part_recv,
    pack_send,
    pack_recv,
):
    nt, nz, nb, tb, n_all, taps, fz, cz, halo, exchange = cfg
    tile = lax.axis_index("tile")
    chan = lax.axis_index("chan")
    beam = lax.axis_index("beam")
    rows_t = n_all * 4
    held_t = n_all * 2

    def peer(t, z, b):
        return {"tile": t, "chan": z, "beam": b}

    order = sorted(range(1, nt), key=lambda d: abs(2 * d - nt)) + [0]
    barrier = pltpu.get_barrier_semaphore()
    count = 0
    for dt in range(nt):
        for dz in range(nz):
            if dt or dz:
                pl.semaphore_signal(
                    barrier,
                    inc=1,
                    device_id=peer(lax.rem(tile + dt, nt), lax.rem(chan + dz, nz), beam),
                    device_id_type=MESH,
                )
                count += 1
    for db in range(1, nb):
        pl.semaphore_signal(
            barrier, inc=1, device_id=peer(tile, chan, lax.rem(beam + db, nb)), device_id_type=MESH
        )
        count += 1

    small = [
        pltpu.make_async_copy(src, dst, small_sem.at[i])
        for i, (src, dst) in enumerate(
            [
                (flag_src, flag_ref),
                (point_src, point_ref),
                (delay_src, delay_ref),
                (chan_src, chan_ref),
                (synth_src, synth_ref),
                (perm_src, perm_ref),
            ]
        )
    ]
    own_loads = [
        pltpu.make_async_copy(
            gain_ref.at[:, :, pl.ds(c * LANES, LANES)], own_gain.at[c], own_sem.at[c]
        )
        for c in range(cz)
    ]
    for load in own_loads + small[:4]:
        load.start()
    loads = []
    for slot, d in enumerate(order):
        block = lax.rem(tile + d, nt)
        loads.append(
            [
                pltpu.make_async_copy(
                    volt_ref.at[pl.ds(block * (tb * held_t), tb * held_t), :, pl.ds(c * LANES, LANES)],
                    volt.at[slot, c],
                    volt_sem.at[slot, c],
                )
                for c in range(cz)
            ]
        )
    for load in loads[0]:
        load.start()
    volt_rows = volt.reshape(nt, cz, tb * rows_t, LANES)
    own_rows = own_gain.reshape(cz, own_gain.shape[1] * 2, LANES)

    for group in loads[1:]:
        for load in group:
            load.start()
    tables = [
        pltpu.make_async_copy(dfth_ref, dft_h, table_sem.at[0]),
        pltpu.make_async_copy(dftl_ref, dft_l, table_sem.at[1]),
    ]
    for copy in small[4:] + tables:
        copy.start()

    row = lax.broadcasted_iota(jnp.int32, (8, LANES), 0)
    first = row < 4
    n_own = n_all // nb
    share = n_own * 4 if exchange else rows_t
    even = lax.rem(lax.broadcasted_iota(jnp.int32, (share, LANES), 0), 2) == 0

    for load in own_loads + small[:1]:
        load.wait()
    if exchange:
        use = jnp.concatenate(
            [
                jnp.where(first, flag_ref[2 * i].astype(F32), flag_ref[2 * i + 1].astype(F32))
                for i in range(n_own // 2)
            ],
            axis=0,
        )
        for c in range(cz):
            gains[beam, c] = use * own_rows[c]

    for h in range(1, halo + 1):

        @pl.when(tile < h)
        def _():
            inbox[h] = jnp.zeros(inbox.shape[1:], F32)

    pl.semaphore_wait(barrier, count)

    gain_copies = []
    if exchange:
        for db in range(1, nb):
            copy = pltpu.make_async_remote_copy(
                src_ref=gains.at[beam],
                dst_ref=gains.at[beam],
                send_sem=gain_send.at[db - 1],
                recv_sem=gain_recv.at[db - 1],
                device_id=peer(tile, chan, lax.rem(beam + db, nb)),
                device_id_type=MESH,
            )
            copy.start()
            gain_copies.append(copy)

    for copy in small[1:4]:
        copy.wait()
    select = lax.broadcasted_iota(jnp.int32, delay_ref.shape, 1) == point_ref[0]
    delay = jnp.sum(jnp.where(select, delay_ref[...], 0.0), axis=1, keepdims=True)
    delay = jnp.broadcast_to(delay, (n_all, LANES))
    delay = jnp.concatenate(
        [
            jnp.where(
                first,
                jnp.broadcast_to(delay[2 * i : 2 * i + 1], (8, LANES)),
                jnp.broadcast_to(delay[2 * i + 1 : 2 * i + 2], (8, LANES)),
            )
            for i in range(n_all // 2)
        ],
        axis=0,
    )
    for c in range(cz):
        frequency = (chan_ref[pl.ds(c, 1), :] + (chan * fz).astype(F32) + 0.5) / (COARSE * nz * fz)
        cycles = delay * frequency
        turn = cycles - jnp.floor(cycles + 0.5)
        square = turn * turn
        w_re[c] = horner(COS_COEF, square)
        w_im[c] = turn * horner(SIN_COEF, square)

    def weigh(start, gain_of):
        rows = pl.ds(start, share)
        for c in range(cz):
            gain = gain_of(c)
            swapped = jnp.where(even, pltpu.roll(gain, share - 1, 0), -pltpu.roll(gain, 1, 0))
            weight = gain * w_re[c, rows, :] + swapped * w_im[c, rows, :]
            w_re[c, rows, :] = jnp.where(even, weight, pltpu.roll(weight, 1, 0))
            w_im[c, rows, :] = jnp.where(even, pltpu.roll(weight, share - 1, 0), weight)

    unroll = 2
    kept = cz * 2 * 8

    def accumulate(slot, starts, extend):
        def step(s, carry):
            for c in range(cz):
                sums = [[jnp.zeros((16, LANES), F32)] * 2 for _ in range(unroll)]
                for start in starts:
                    for q in range(share // 16):
                        at = start + q * 16
                        wr = w_re[c, pl.ds(at, 16), :]
                        wi = w_im[c, pl.ds(at, 16), :]
                        for u in range(unroll):
                            begin = pl.multiple_of((s * unroll + u) * rows_t + at, 16)
                            v = volt_rows[slot, c, pl.ds(begin, 16), :].astype(F32)
                            sums[u] = [sums[u][0] + wr * v, sums[u][1] + wi * v]
                for u in range(unroll):
                    begin = pl.multiple_of((s * unroll + u) * kept, 8)
                    for which in range(2):
                        value = sums[u][which]
                        value = value[:8] + value[8:]
                        rows = pl.ds(begin + (c * 2 + which) * 8, 8)
                        acc[slot, rows, :] = acc[slot, rows, :] + value if extend else value
            return carry

        lax.fori_loop(0, tb // unroll, step, 0)

    starts = [0]
    if exchange:
        starts = [pl.multiple_of(lax.rem(beam + db, nb) * share, 16) for db in range(nb)]
        weigh(starts[0], lambda c: gains[beam, c])
        for slot in range(nt):
            for load in loads[slot]:
                load.wait()
            accumulate(slot, starts[:1], False)
        for copy in gain_copies:
            copy.wait_recv()
        for db in range(1, nb):
            weigh(starts[db], lambda c, db=db: gains[lax.rem(beam + db, nb), c])
    else:
        weigh(0, lambda c: own_rows[c])
    part_copies = []
    for slot, d in enumerate(order):
        if exchange:
            accumulate(slot, starts[1:], True)
        else:
            for load in loads[slot]:
                load.wait()
            accumulate(slot, starts, False)

        def take(which, p, c, ri):
            total = None
            for half in range(2):
                start = (c * 2 + which) * 8 + half * 4 + p * 2 + ri
                value = acc[slot, pl.ds(start, tb, stride=kept), :]
                total = value if total is None else total + value
            return total

        for p in range(2):
            for c in range(cz):
                part[slot, p * 2 * cz + c] = take(0, p, c, 0) - take(1, p, c, 1)
                part[slot, (p * 2 + 1) * cz + c] = take(0, p, c, 1) + take(1, p, c, 0)
        if d:
            copy = pltpu.make_async_remote_copy(
                src_ref=part.at[slot],
                dst_ref=recv.at[slot],
                send_sem=part_send.at[slot],
                recv_sem=part_recv.at[slot],
                device_id=peer(lax.rem(tile + d, nt), chan, beam),
                device_id_type=MESH,
            )
            copy.start()
            part_copies.append(copy)

    for copy in part_copies:
        copy.wait_recv()

    def total_of(g, c):
        value = part[nt - 1, g * cz + c]
        for slot in range(nt - 1):
            value = value + recv[slot, g * cz + c]
        return value

    sums = jnp.concatenate(
        [jnp.concatenate([total_of(g, c) for c in range(cz)], axis=1) for g in range(4)], axis=0
    )
    high = sums.astype(BF16)
    low = (sums - high.astype(F32)).astype(BF16)
    for copy in small[4:]:
        copy.wait()
    table = perm_ref[...]
    moved = jnp.dot(high, table, preferred_element_type=F32) + jnp.dot(
        low, table, preferred_element_type=F32
    )
    group = lax.broadcasted_iota(jnp.int32, (tb, LANES), 1) // fz
    for z in range(nz):
        for c in range(cz):
            total = None
            for g in range(4):
                value = moved[g * tb : (g + 1) * tb, c * LANES : (c + 1) * LANES]
                shift = (g - z) * fz % LANES
                if shift:
                    value = pltpu.roll(value, shift, 1)
                total = value if g == 0 else jnp.where(group == g, value, total)
            packed[z, c] = total

    def pack_copy(h, dz):
        return pltpu.make_async_remote_copy(
            src_ref=packed.at[lax.rem(chan + dz, nz)],
            dst_ref=inbox.at[h, chan],
            send_sem=pack_send.at[h, dz],
            recv_sem=pack_recv.at[h, dz],
            device_id=peer(lax.rem(tile + h, nt), lax.rem(chan + dz, nz), beam),
            device_id_type=MESH,
        )

    spread = sorted(range(nz), key=lambda d: abs(2 * d - nz))
    for h in range(halo + 1):
        for dz in spread:
            if h == 0 and dz == 0:
                continue
            if h == 0:
                pack_copy(h, dz).start()
            else:

                @pl.when(tile + h < nt)
                def _():
                    pack_copy(h, dz).start()

    inbox[0, chan] = packed[chan]

    for copy in tables:
        copy.wait()
    for h in range(halo + 1):
        for dz in range(nz):
            if h == 0 and dz == 0:
                continue
            if h == 0:
                pack_copy(h, dz).wait_recv()
            else:

                @pl.when(tile >= h)
                def _():
                    pack_copy(h, dz).wait_recv()

    lhs = jnp.concatenate(
        [
            jnp.concatenate([inbox[h, z, c] for z in range(nz)], axis=1)
            for c in range(cz)
            for h in range(halo, -1, -1)
        ],
        axis=0,
    )
    high = lhs.astype(BF16)
    low = (lhs - high.astype(F32)).astype(BF16)
    spec[...] = (
        jnp.dot(high, dft_h[...], preferred_element_type=F32)
        + jnp.dot(low, dft_h[...], preferred_element_type=F32)
        + jnp.dot(high, dft_l[...], preferred_element_type=F32)
    )
    span = (halo + 1) * tb
    for c in range(cz):
        for g in range(4):
            total = None
            for k in range(taps):
                value = synth_ref[pl.ds(k, 1), :] * spec[
                    pl.ds(c * span + halo * tb - k, tb), g * LANES : (g + 1) * LANES
                ]
                total = value if total is None else total + value
            out_ref[c, :, g * LANES : (g + 1) * LANES] = total

    for copy in gain_copies:
        copy.wait_send()
    for copy in part_copies:
        copy.wait_send()
    for h in range(halo + 1):
        for dz in range(nz):
            if h == 0 and dz == 0:
                continue
            if h == 0:
                pack_copy(h, dz).wait_send()
            else:

                @pl.when(tile + h < nt)
                def _():
                    pack_copy(h, dz).wait_send()


def body(mesh, voltages, calib_gain, tile_flags, delays, pointing, synth_filter):
    nt, nz, nb = mesh.shape["tile"], mesh.shape["chan"], mesh.shape["beam"]
    total_rows, n_all = voltages.shape[:2]
    width = voltages.shape[-1]
    taps, k = synth_filter.shape
    tb = total_rows // nt
    fz = width // COARSE
    cz = COARSE // nz
    halo = -(-(taps - 1) // tb)
    n_own = calib_gain.shape[0]
    exchange = n_own % 4 == 0 and mesh.shape["beam"] > 1
    gain = calib_gain
    if not exchange:
        gain = gain * tile_flags.astype(F32)[:, None, None, None]
        gain = lax.all_gather(gain, "beam", axis=0, tiled=True)
    local = np.arange(width).reshape(-1, LANES)
    channel = (local % COARSE * k + local // COARSE).astype(np.float32)
    dft_h, dft_l = dft_table(nz, fz)
    perm = gather_table(nz, fz, cz)
    cfg = (nt, nz, nb, tb, n_all, taps, fz, cz, halo, exchange)
    vmem = pl.BlockSpec(memory_space=pltpu.VMEM)
    anywhere = pl.BlockSpec(memory_space=pl.ANY)
    span = (halo + 1) * tb
    dma = pltpu.SemaphoreType.DMA
    out = pl.pallas_call(
        functools.partial(kernel, cfg),
        out_shape=jax.ShapeDtypeStruct((cz, tb, 4 * k), F32),
        in_specs=[anywhere] * 10,
        out_specs=vmem,
        scratch_shapes=[
            pltpu.SMEM(tile_flags.shape, jnp.int32),
            pltpu.VMEM(delays.shape[::-1], F32),
            pltpu.SMEM(pointing.shape, jnp.int32),
            pltpu.VMEM(synth_filter.shape, F32),
            pltpu.VMEM(channel.shape, F32),
            pltpu.VMEM(perm.shape, BF16),
            dma((6,)),
            pltpu.VMEM((nt, cz, tb * n_all * 2, 2, LANES), BF16),
            pltpu.VMEM((cz, gain.shape[0] * 2, 2, LANES), F32),
            pltpu.VMEM((nb, cz, n_own * 4, LANES), F32),
            pltpu.VMEM((cz, n_all * 4, LANES), F32),
            pltpu.VMEM((cz, n_all * 4, LANES), F32),
            pltpu.VMEM((nt, tb * cz * 16, LANES), F32),
            pltpu.VMEM((nt, 4 * cz, tb, LANES), F32),
            pltpu.VMEM((nt - 1, 4 * cz, tb, LANES), F32),
            pltpu.VMEM((nz, cz, tb, LANES), F32),
            pltpu.VMEM((halo + 1, nz, cz, tb, LANES), F32),
            pltpu.VMEM((cz * span, 4 * k), F32),
            pltpu.VMEM(dft_h.shape, BF16),
            pltpu.VMEM(dft_l.shape, BF16),
            dma((nt, cz)),
            dma((2,)),
            dma((cz,)),
            dma((max(nb - 1, 1),)),
            dma((max(nb - 1, 1),)),
            dma((nt,)),
            dma((nt,)),
            dma((halo + 1, nz)),
            dma((halo + 1, nz)),
        ],
        compiler_params=pltpu.CompilerParams(collective_id=0, has_side_effects=True),
    )(
        voltages.reshape(-1, 2, width),
        gain.reshape(-1, 2, width),
        tile_flags,
        delays.T,
        pointing,
        synth_filter,
        jnp.asarray(channel),
        jnp.asarray(perm),
        jnp.asarray(dft_h),
        jnp.asarray(dft_l),
    )
    return out.reshape(cz, tb, 2, 2 * k).transpose(1, 2, 0, 3)[:, None]


def solution(mesh):
    in_specs = (
        P(None, "tile", None, None, "chan"),
        P(("tile", "beam"), None, None, "chan"),
        P(("tile", "beam")),
        P(None, "tile"),
        P("beam"),
        P(),
    )
    out_specs = P("tile", "beam", None, "chan", None)
    return jax.shard_map(
        functools.partial(body, mesh), mesh=mesh, in_specs=in_specs, out_specs=out_specs, check_vma=False
    )
```

profile of v0, /device:TPU:0, one launch (start us, length us, event | category | flops | bytes accessed | tf_op | source)
XLA Modules:
  0.0 21.6 jit_solution(18421567386395242997)
XLA Ops:
  0.7 19.5 %shard_map.100 = f32[3,8,512]{2,1,0:T(8,128)} custom-call(bf16[2048,2,384]{2,1,0:T(2,128)(2,1)} %bitcast.9, f32[32,2,384]{2,1,0:T(2,128)} %bitcast.11, s32[16]{0:T(128)} %flag_src.1, f32[32,64]{1,0:T(8,128)} %bitcast.12, s32[1]{0:T(128)S(6)} %copy.14.point_src, f32[12,128]{1,0:T(8,128)} %synth_src.1, f32[3,128]{1,0:T(4,128)} %constant.8.clone.chan_src, ...), custom_call_target="tpu_custom_call" | custom-call | tf_op jit(solution)/shard_map/pallas_call | solution.py:475
  20.1 1.4 %copy.13 = f32[3,8,2,256]{3,2,0,1:T(2,128)} copy(f32[3,8,2,256]{3,1,2,0:T(8,128)} %bitcast.10) | data formatting | bytes 98304 | tf_op jit(solution)/shard_map/reshape | solution.py:524
where the time goes:
time: 21.9 us; the launch traced here: 21.6 us
  Pallas kernels  19.5 us (89%)
  local copies, waits for them, and re-layouts  1.44 us (7%)
  between operations  0.66 us (3%)
    pallas_call x1, Pallas kernels, body(): pl.pallas_call(functools.partial(kernel, cfg), out_shape=jax.ShapeDtypeSt...  19.5 us
    reshape x1, local copies, waits for them, and re-layouts, body(): return out.reshape(cz, tb, 2, 2 * k).transpose(1, 2, 0, 3)[:, None]  1.44 us

commit v1 on v0

v1 whole, which is shorter than its diff:
```python
import functools
import math

import jax
import jax.numpy as jnp
import numpy as np
from jax import lax
from jax.experimental import pallas as pl
from jax.experimental.pallas import tpu as pltpu
from jax.sharding import PartitionSpec as P

COARSE = 12
LANES = 128
MESH = pl.DeviceIdType.MESH
F32 = jnp.float32
BF16 = jnp.bfloat16


def even_fit(func, degree):
    series = np.polynomial.chebyshev.Chebyshev.interpolate(
        lambda u: func(np.sqrt(u)), degree, domain=[0.0, 0.25]
    )
    return [float(v) for v in series.convert(kind=np.polynomial.Polynomial).coef]


COS_COEF = even_fit(lambda r: np.cos(2 * np.pi * r), 7)
SIN_COEF = even_fit(lambda r: 2 * np.pi * np.sinc(2 * r), 7)


def horner(coef, u):
    total = jnp.full_like(u, coef[-1])
    for value in coef[-2::-1]:
        total = total * u + value
    return total


def split_bf16(table):
    high = table.astype(BF16)
    low = (table - high.astype(np.float64)).astype(BF16)
    return high, low


def dft_table(nz, fz):
    k = nz * fz
    f = np.arange(k)
    m = np.arange(k)
    angle = 2 * np.pi * (f[:, None] * m[None, :] % k) / k
    cosine, sine = np.cos(angle) / math.sqrt(k), np.sin(angle) / math.sqrt(k)
    out = np.zeros((nz, 2, 2, fz, 2, 2, k))
    for p in range(2):
        out[:, p, 0, :, p, 0] = cosine.reshape(nz, fz, k)
        out[:, p, 0, :, p, 1] = sine.reshape(nz, fz, k)
        out[:, p, 1, :, p, 0] = -sine.reshape(nz, fz, k)
        out[:, p, 1, :, p, 1] = cosine.reshape(nz, fz, k)
    return split_bf16(out.reshape(nz * 4 * fz, 4 * k))


def gather_table(nz, fz, cz):
    width = fz * COARSE
    out = np.zeros((width, width), np.float64)
    for c in range(cz):
        for z in range(nz):
            for f in range(fz):
                out[f * COARSE + z * cz + c, (c * nz + z) * fz + f] = 1.0
    return out.astype(BF16)


def kernel(
    cfg,
    volt_ref,
    gain_ref,
    flag_src,
    delay_src,
    point_src,
    synth_src,
    table_src,
    out_ref,
    flag_ref,
    delay_ref,
    point_ref,
    synth_ref,
    table_ref,
    volt,
    own_gain,
    gains,
    w_re,
    w_im,
    acc,
    part,
    recv,
    packed,
    inbox,
    spec,
    small_sem,
    own_sem,
    volt_sem,
    gain_send,
    gain_recv,
    part_send,
    part_recv,
    pack_send,
    pack_recv,
):
    nt, nz, nb, tb, n_all, taps, fz, cz, halo, exchange = cfg
    tile = lax.axis_index("tile")
    chan = lax.axis_index("chan")
    beam = lax.axis_index("beam")
    rows_t = n_all * 4

    def peer(t, z, b):
        return {"tile": t, "chan": z, "beam": b}

    pair = 2 if nt % 2 == 0 else 1
    chips = nt // pair
    chip, core = lax.div(tile, pair), lax.rem(tile, pair)
    order = [
        (a, k)
        for a in sorted(range(1, chips), key=lambda a: abs(2 * a - chips))
        for k in range(pair)
    ] + [(0, k) for k in range(pair - 1, -1, -1)]

    def time_block(slot):
        a, k = order[slot]
        return lax.rem(chip + a, chips) * pair + lax.rem(core + k, pair)

    def wait_all(ref, sem):
        pltpu.make_async_copy(ref, ref, sem).wait()

    gain_rows = gain_ref.reshape(gain_ref.shape[0] * 2, gain_ref.shape[2])
    for c in range(cz):
        pltpu.make_async_copy(
            gain_rows.at[:, pl.ds(c * LANES, LANES)], own_gain.at[c], own_sem.at[0]
        ).start()
    small = [
        pltpu.make_async_copy(src, dst, small_sem.at[i])
        for i, (src, dst) in enumerate(
            [
                (flag_src, flag_ref),
                (point_src, point_ref),
                (delay_src, delay_ref),
                (synth_src, synth_ref),
                (table_src, table_ref),
            ]
        )
    ]
    for copy in small[:3]:
        copy.start()

    barrier = pltpu.get_barrier_semaphore()
    count = 0
    for dt in range(nt):
        for dz in range(nz):
            if dt or dz:
                pl.semaphore_signal(
                    barrier,
                    inc=1,
                    device_id=peer(lax.rem(tile + dt, nt), lax.rem(chan + dz, nz), beam),
                    device_id_type=MESH,
                )
                count += 1
    for db in range(1, nb):
        pl.semaphore_signal(
            barrier, inc=1, device_id=peer(tile, chan, lax.rem(beam + db, nb)), device_id_type=MESH
        )
        count += 1

    volt_rows = volt_ref.reshape(volt_ref.shape[0] * 2, volt_ref.shape[2])
    for c in range(cz):
        for slot in range(nt):
            pltpu.make_async_copy(
                volt_rows.at[
                    pl.ds(time_block(slot) * (tb * rows_t), tb * rows_t), pl.ds(c * LANES, LANES)
                ],
                volt.at[slot, c],
                volt_sem.at[c],
            ).start()
    for copy in small[3:]:
        copy.start()

    row = lax.broadcasted_iota(jnp.int32, (8, LANES), 0)
    first = row < 4
    n_own = n_all // nb
    share = n_own * 4 if exchange else rows_t
    even = lax.rem(lax.broadcasted_iota(jnp.int32, (share, LANES), 0), 2) == 0

    with jax.named_scope("ownload"):
        wait_all(own_gain, own_sem.at[0])
        small[0].wait()
    if exchange:
        use = jnp.concatenate(
            [
                jnp.where(first, flag_ref[2 * i].astype(F32), flag_ref[2 * i + 1].astype(F32))
                for i in range(n_own // 2)
            ],
            axis=0,
        )
        for c in range(cz):
            gains[beam, c] = use * own_gain[c]

    for h in range(1, halo + 1):

        @pl.when(tile < h)
        def _():
            inbox[h] = jnp.zeros(inbox.shape[1:], F32)

    unused = halo * tb - (taps - 1)
    if unused:
        inbox[halo, :, :, pl.ds(0, unused), :] = jnp.zeros((nz, cz, unused, LANES), F32)

    with jax.named_scope("barrier"):
        pl.semaphore_wait(barrier, count)

    if exchange:
        for c in range(cz):
            for db in range(1, nb):
                pltpu.make_async_remote_copy(
                    src_ref=gains.at[beam, c],
                    dst_ref=gains.at[beam, c],
                    send_sem=gain_send.at[0],
                    recv_sem=gain_recv.at[c],
                    device_id=peer(tile, chan, lax.rem(beam + db, nb)),
                    device_id_type=MESH,
                ).start()

    for copy in small[1:3]:
        copy.wait()
    select = lax.broadcasted_iota(jnp.int32, delay_ref.shape, 1) == point_ref[0]
    delay = jnp.sum(jnp.where(select, delay_ref[...], 0.0), axis=1, keepdims=True)
    delay = jnp.broadcast_to(delay, (n_all, LANES))
    delay = jnp.concatenate(
        [
            jnp.where(
                first,
                jnp.broadcast_to(delay[2 * i : 2 * i + 1], (8, LANES)),
                jnp.broadcast_to(delay[2 * i + 1 : 2 * i + 2], (8, LANES)),
            )
            for i in range(n_all // 2)
        ],
        axis=0,
    )
    for c in range(cz):
        local = (lax.broadcasted_iota(jnp.int32, (1, LANES), 1) + c * LANES).astype(F32)
        fine = jnp.floor((local + 0.5) / COARSE)
        channel = (local - COARSE * fine) * (nz * fz) + fine + (chan * fz).astype(F32)
        frequency = (channel + 0.5) / (COARSE * nz * fz)
        cycles = delay * frequency
        turn = cycles - jnp.floor(cycles + 0.5)
        square = turn * turn
        w_re[c] = horner(COS_COEF, square)
        w_im[c] = turn * horner(SIN_COEF, square)

    def weigh(c, start, gain):
        rows = pl.ds(start, share)
        swapped = jnp.where(even, pltpu.roll(gain, share - 1, 0), -pltpu.roll(gain, 1, 0))
        weight = gain * w_re[c, rows, :] + swapped * w_im[c, rows, :]
        w_re[c, rows, :] = jnp.where(even, weight, pltpu.roll(weight, 1, 0))
        w_im[c, rows, :] = jnp.where(even, pltpu.roll(weight, share - 1, 0), weight)

    unroll = math.gcd(tb, 8)

    def accumulate(slot, c, starts, extend):
        def step(s, carry):
            sums = [[jnp.zeros((16, LANES), F32)] * 2 for _ in range(unroll)]
            for start in starts:
                for q in range(share // 16):
                    at = start + q * 16
                    wr = w_re[c, pl.ds(at, 16), :]
                    wi = w_im[c, pl.ds(at, 16), :]
                    for u in range(unroll):
                        begin = pl.multiple_of((s * unroll + u) * rows_t + at, 16)
                        v = volt[slot, c, pl.ds(begin, 16), :].astype(F32)
                        sums[u] = [sums[u][0] + wr * v, sums[u][1] + wi * v]
            for u in range(unroll):
                begin = pl.multiple_of((s * unroll + u) * 16, 16)
                for which in range(2):
                    value = sums[u][which]
                    value = value[:8] + value[8:]
                    rows = pl.ds(begin + which * 8, 8)
                    acc[slot, c, rows, :] = acc[slot, c, rows, :] + value if extend else value
            return carry

        if tb == unroll:
            step(0, 0)
        else:
            lax.fori_loop(0, tb // unroll, step, 0)

    def take(slot, c, which, p, ri):
        total = None
        for half in range(2):
            value = acc[slot, c, pl.ds(which * 8 + half * 4 + p * 2 + ri, tb, stride=16), :]
            total = value if total is None else total + value
        return total

    starts = [0]
    if exchange:
        starts = [pl.multiple_of(lax.rem(beam + db, nb) * share, 16) for db in range(nb)]
    with jax.named_scope("acc1"):
        for c in range(cz):
            weigh(c, starts[0], gains[beam, c] if exchange else own_gain[c])
            if exchange:
                wait_all(volt.at[:, c], volt_sem.at[c])

                def first_sum(slot, carry, c=c):
                    accumulate(slot, c, starts[:1], False)
                    return carry

                lax.fori_loop(0, nt, first_sum, 0)
    for c in range(cz):
        with jax.named_scope(f"gainwait{c}"):
            if exchange:
                wait_all(gains.at[pl.ds(0, nb - 1), c], gain_recv.at[c])
            else:
                wait_all(volt.at[:, c], volt_sem.at[c])
        for db in range(1, nb if exchange else 1):
            weigh(c, starts[db], gains[lax.rem(beam + db, nb), c])
        for slot in range(nt):
            if exchange:
                accumulate(slot, c, starts[1:], True)
            else:
                accumulate(slot, c, starts, False)
            for p in range(2):
                part[slot, c, p * 2] = take(slot, c, 0, p, 0) - take(slot, c, 1, p, 1)
                part[slot, c, p * 2 + 1] = take(slot, c, 0, p, 1) + take(slot, c, 1, p, 0)
            if slot < nt - 1:
                pltpu.make_async_remote_copy(
                    src_ref=part.at[slot, c],
                    dst_ref=recv.at[slot, c],
                    send_sem=part_send.at[0],
                    recv_sem=part_recv.at[c],
                    device_id=peer(time_block(slot), chan, beam),
                    device_id_type=MESH,
                ).start()

    for copy in small[3:]:
        copy.wait()
    kdim = 4 * nz * fz
    moved = jnp.zeros((4 * tb, cz * LANES), F32)
    for c in range(cz):
        with jax.named_scope(f"partwait{c}"):
            wait_all(recv.at[:, c], part_recv.at[c])
        sums = part[nt - 1, c]
        for slot in range(nt - 1):
            sums = sums + recv[slot, c]
        sums = sums.reshape(4 * tb, LANES)
        high = sums.astype(BF16)
        low = (sums - high.astype(F32)).astype(BF16)
        table = table_ref[pl.ds(2 * kdim + c * LANES, LANES), pl.ds(0, cz * LANES)]
        moved = moved + jnp.dot(high, table, preferred_element_type=F32)
        moved = moved + jnp.dot(low, table, preferred_element_type=F32)
    group = lax.broadcasted_iota(jnp.int32, (tb, LANES), 1) // fz
    for z in range(nz):
        for c in range(cz):
            total = None
            for g in range(4):
                value = moved[g * tb : (g + 1) * tb, c * LANES : (c + 1) * LANES]
                shift = (g - z) * fz % LANES
                if shift:
                    value = pltpu.roll(value, shift, 1)
                total = value if g == 0 else jnp.where(group == g, value, total)
            packed[z, c] = total

    half = 2 * chan // nz
    place = chan * half + (nz - 1 - chan) * (1 - half)

    def target(i):
        if i == nz - 1:
            return chan
        other = i + (i + nz - place) // nz
        return other * half + (nz - 1 - other) * (1 - half)

    def halo_rows(h):
        count = tb if h < halo else taps - 1 - (halo - 1) * tb
        return pl.ds(tb - count, count)

    messages = [(h, i) for i in range(nz) for h in range(halo + 1) if h or i < nz - 1]

    for h, i in messages:

        def send(h=h, i=i):
            pltpu.make_async_remote_copy(
                src_ref=packed.at[target(i), :, halo_rows(h), :],
                dst_ref=inbox.at[h, chan, :, halo_rows(h), :],
                send_sem=pack_send.at[h],
                recv_sem=pack_recv.at[h],
                device_id=peer(lax.rem(tile + h, nt), target(i), beam),
                device_id_type=MESH,
            ).start()

        if h == 0:
            send()
        else:
            pl.when(tile + h < nt)(send)

    inbox[0, chan] = packed[chan]

    with jax.named_scope("packwait"):
        for h in range(halo + 1):
            if h == 0:
                wait_all(inbox.at[0, pl.ds(0, nz - 1)], pack_recv.at[0])
            else:

                @pl.when(tile >= h)
                def _():
                    wait_all(inbox.at[h, :, :, halo_rows(h), :], pack_recv.at[h])

    lhs = jnp.concatenate(
        [
            jnp.concatenate([inbox[h, z, c] for z in range(nz)], axis=1)
            for c in range(cz)
            for h in range(halo, -1, -1)
        ],
        axis=0,
    )
    high = lhs.astype(BF16)
    low = (lhs - high.astype(F32)).astype(BF16)
    spec[...] = (
        jnp.dot(high, table_ref[pl.ds(0, kdim), :], preferred_element_type=F32)
        + jnp.dot(low, table_ref[pl.ds(0, kdim), :], preferred_element_type=F32)
        + jnp.dot(high, table_ref[pl.ds(kdim, kdim), :], preferred_element_type=F32)
    )
    span = (halo + 1) * tb
    for c in range(cz):
        for g in range(4):
            total = None
            for k in range(taps):
                value = synth_ref[pl.ds(k, 1), :] * spec[
                    pl.ds(c * span + halo * tb - k, tb), g * LANES : (g + 1) * LANES
                ]
                total = value if total is None else total + value
            for t in range(tb):
                out_ref[t, c, pl.ds(g // 2, 1), (g % 2) * LANES : (g % 2 + 1) * LANES] = total[t : t + 1]

    with jax.named_scope("sendwait"):
        if exchange:
            wait_all(gains.at[pl.ds(0, nb - 1)], gain_send.at[0])
        wait_all(recv, part_send.at[0])
        for h in range(halo + 1):
            if h == 0:
                wait_all(packed.at[pl.ds(0, nz - 1)], pack_send.at[0])
            else:

                @pl.when(tile + h < nt)
                def _():
                    wait_all(packed.at[:, :, halo_rows(h), :], pack_send.at[h])


def store(value_ref, out_ref, sem):
    copy = pltpu.make_async_copy(value_ref, out_ref, sem)
    copy.start()
    copy.wait()


def body(mesh, voltages, calib_gain, tile_flags, delays, pointing, synth_filter):
    nt, nz, nb = mesh.shape["tile"], mesh.shape["chan"], mesh.shape["beam"]
    total_rows, n_all = voltages.shape[:2]
    width = voltages.shape[-1]
    taps, k = synth_filter.shape
    tb = total_rows // nt
    fz = width // COARSE
    cz = COARSE // nz
    halo = -(-(taps - 1) // tb)
    n_own = calib_gain.shape[0]
    exchange = n_own % 4 == 0 and mesh.shape["beam"] > 1
    gain = calib_gain
    if not exchange:
        gain = gain * tile_flags.astype(F32)[:, None, None, None]
        gain = lax.all_gather(gain, "beam", axis=0, tiled=True)
    perm = gather_table(nz, fz, cz)
    perm = np.pad(perm, ((0, 0), (0, 4 * k - perm.shape[1])))
    table = np.concatenate([*dft_table(nz, fz), perm])
    cfg = (nt, nz, nb, tb, n_all, taps, fz, cz, halo, exchange)
    vmem = pl.BlockSpec(memory_space=pltpu.VMEM)
    anywhere = pl.BlockSpec(memory_space=pltpu.HBM)
    span = (halo + 1) * tb
    dma = pltpu.SemaphoreType.DMA
    out = pl.pallas_call(
        functools.partial(kernel, cfg),
        out_shape=pltpu.VMEM((tb, cz, 2, 2 * k), F32),
        in_specs=[anywhere] * 7,
        out_specs=vmem,
        scratch_shapes=[
            pltpu.SMEM(tile_flags.shape, jnp.int32),
            pltpu.VMEM(delays.shape[::-1], F32),
            pltpu.SMEM(pointing.shape, jnp.int32),
            pltpu.VMEM(synth_filter.shape, F32),
            pltpu.VMEM(table.shape, BF16),
            pltpu.VMEM((nt, cz, tb * n_all * 4, LANES), BF16),
            pltpu.VMEM((cz, gain.shape[0] * 4, LANES), F32),
            pltpu.VMEM((nb, cz, n_own * 4, LANES), F32),
            pltpu.VMEM((cz, n_all * 4, LANES), F32),
            pltpu.VMEM((cz, n_all * 4, LANES), F32),
            pltpu.VMEM((nt, cz, tb * 16, LANES), F32),
            pltpu.VMEM((nt, cz, 4, tb, LANES), F32),
            pltpu.VMEM((nt - 1, cz, 4, tb, LANES), F32),
            pltpu.VMEM((nz, cz, tb, LANES), F32),
            pltpu.VMEM((halo + 1, nz, cz, tb, LANES), F32),
            pltpu.VMEM((cz * span, 4 * k), F32),
            dma((5,)),
            dma((1,)),
            dma((cz,)),
            dma((1,)),
            dma((cz,)),
            dma((1,)),
            dma((cz,)),
            dma((halo + 1,)),
            dma((halo + 1,)),
        ],
        compiler_params=pltpu.CompilerParams(collective_id=0, has_side_effects=True),
    )(
        voltages.reshape(-1, 2, width),
        gain.reshape(-1, 2, width),
        tile_flags,
        delays.T,
        pointing,
        synth_filter,
        jnp.asarray(table),
    )
    final = pl.pallas_call(
        store,
        out_shape=jax.ShapeDtypeStruct(out.shape, F32),
        in_specs=[vmem],
        out_specs=pl.BlockSpec(memory_space=pltpu.HBM),
        scratch_shapes=[dma(())],
    )(pltpu.with_memory_space_constraint(out, pltpu.VMEM))
    return final.transpose(0, 2, 1, 3)[:, None]


def solution(mesh):
    in_specs = (
        P(None, "tile", None, None, "chan"),
        P(("tile", "beam"), None, None, "chan"),
        P(("tile", "beam")),
        P(None, "tile"),
        P("beam"),
        P(),
    )
    out_specs = P("tile", "beam", None, "chan", None)
    return jax.shard_map(
        functools.partial(body, mesh), mesh=mesh, in_specs=in_specs, out_specs=out_specs, check_vma=False
    )
```

time: 21.9 us -> 18.4 us (0.84)
  Pallas kernels: 19.5 us -> 17.6 us
  local copies, waits for them, and re-layouts: 1.44 us -> 0 us
    pallas_call x1 -> x2, Pallas kernels: 19.5 us -> 17.6 us  [the longest x1 17 us: body(): pl.pallas_call(functools.partial(kernel, cfg), out_shape=pltpu.VMEM((tb,...]
    reshape x1 -> x0, local copies, waits for them, and re-layouts: 1.44 us -> none  [body(): return out.reshape(cz, tb, 2, 2 * k).transpose(1, 2, 0, 3)[:, None]]
where the time goes in v1:
time: 18.4 us; the launch traced here: 18.2 us
  Pallas kernels  17.6 us (96%)
  between operations  0.66 us (4%)
    pallas_call x1, Pallas kernels, body(): pl.pallas_call(functools.partial(kernel, cfg), out_shape=pltpu.VMEM((tb,...  17 us
    pallas_call x1, Pallas kernels, body(): pl.pallas_call(store, out_shape=jax.ShapeDtypeStruct(out.shape, F32), in_...  0.63 us

profile of v1, /device:TPU:0, one launch (start us, length us, event | category | flops | bytes accessed | tf_op | source)
XLA Modules:
  0.0 18.2 jit_solution(5587609158927763165)
XLA Ops:
  0.7 17.0 %shard_map.73.value_ref = f32[8,3,2,256]{3,2,1,0:T(2,128)S(1)} custom-call(bf16[2048,2,384]{2,1,0:T(2,128)(2,1)} %bitcast.8, f32[32,2,384]{2,1,0:T(2,128)} %bitcast.9, s32[16]{0:T(128)} %flag_src.1, f32[32,64]{1,0:T(8,128)} %bitcast.10, s32[1]{0:T(128)S(6)} %copy.9.point_src, f32[12,128]{1,0:T(8,128)} %synth_src.1, bf16[1408,512]{1,0:T(8,128)(2,1)} %constant.2.clone.table_src), custom_call_target="tpu_custom_call" | custom-call | tf_op jit(solution)/shard_map/pallas_call | solution.py:476
  17.6 0.6 %shard_map.74 = f32[8,3,2,256]{3,2,1,0:T(2,128)} custom-call(f32[8,3,2,256]{3,2,1,0:T(2,128)S(1)} %shard_map.73.value_ref), custom_call_target="tpu_custom_call" | custom-call | tf_op jit(solution)/shard_map/pallas_call | solution.py:518

commit v2 on v1

--- a/solution.py
+++ b/solution.py
@@ -73,13 +73,15 @@
     delay_src,
     point_src,
     synth_src,
-    table_src,
+    perm_src,
+    dft_src,
     out_ref,
     flag_ref,
     delay_ref,
     point_ref,
     synth_ref,
-    table_ref,
+    perm_ref,
+    dft_ref,
     volt,
     own_gain,
     gains,
@@ -100,6 +102,7 @@
     part_recv,
     pack_send,
     pack_recv,
+    dft_sem,
 ):
     nt, nz, nb, tb, n_all, taps, fz, cz, halo, exchange = cfg
     tile = lax.axis_index("tile")
@@ -113,15 +116,16 @@
     pair = 2 if nt % 2 == 0 else 1
     chips = nt // pair
     chip, core = lax.div(tile, pair), lax.rem(tile, pair)
-    order = [
-        (a, k)
-        for a in sorted(range(1, chips), key=lambda a: abs(2 * a - chips))
-        for k in range(pair)
-    ] + [(0, k) for k in range(pair - 1, -1, -1)]
-
-    def time_block(slot):
-        a, k = order[slot]
-        return lax.rem(chip + a, chips) * pair + lax.rem(core + k, pair)
+    packer = pair - 1
+    packs = core == packer
+    order = sorted(range(1, chips), key=lambda a: abs(2 * a - chips)) + [0]
+    block = pair * tb
+
+    def chip_of(slot):
+        return lax.rem(chip + order[slot], chips)
+
+    def packer_of(target_chip):
+        return target_chip * pair + packer
 
     def wait_all(ref, sem):
         pltpu.make_async_copy(ref, ref, sem).wait()
@@ -139,42 +143,63 @@
                 (point_src, point_ref),
                 (delay_src, delay_ref),
                 (synth_src, synth_ref),
-                (table_src, table_ref),
+                (perm_src, perm_ref),
             ]
         )
     ]
+    dft_copies = [
+        pltpu.make_async_copy(
+            dft_src.at[:, g], dft_ref.at[:, lax.rem(chan + g, 4)], dft_sem.at[0]
+        )
+        for g in range(4)
+    ]
     for copy in small[:3]:
         copy.start()
 
     barrier = pltpu.get_barrier_semaphore()
-    count = 0
-    for dt in range(nt):
-        for dz in range(nz):
-            if dt or dz:
-                pl.semaphore_signal(
-                    barrier,
-                    inc=1,
-                    device_id=peer(lax.rem(tile + dt, nt), lax.rem(chan + dz, nz), beam),
-                    device_id_type=MESH,
-                )
-                count += 1
+
+    def greet(t, z, b):
+        pl.semaphore_signal(barrier, inc=1, device_id=peer(t, z, b), device_id_type=MESH)
+
     for db in range(1, nb):
-        pl.semaphore_signal(
-            barrier, inc=1, device_id=peer(tile, chan, lax.rem(beam + db, nb)), device_id_type=MESH
-        )
-        count += 1
+        greet(tile, chan, lax.rem(beam + db, nb))
+    if pair > 1:
+
+        @pl.when(packs)
+        def _():
+            for a in range(chips):
+                for k in range(packer):
+                    greet(lax.rem(chip + a, chips) * pair + k, chan, beam)
+
+        @pl.when(jnp.logical_not(packs))
+        def _():
+            for a in range(chips):
+                greet(packer_of(lax.rem(chip + a, chips)), chan, beam)
+
+    for dz in range(nz):
+        for a in range(chips):
+            if dz == 0:
+                if a:
+                    pl.when(packs)(
+                        functools.partial(greet, packer_of(lax.rem(chip + a, chips)), chan, beam)
+                    )
+            else:
+                greet(packer_of(lax.rem(chip + a, chips)), lax.rem(chan + dz, nz), beam)
+
+    few = chips * (pair - 1) // max(packer, 1) + nb - 1
+    many = nt * nz - 1 + nb - 1
 
     volt_rows = volt_ref.reshape(volt_ref.shape[0] * 2, volt_ref.shape[2])
     for c in range(cz):
-        for slot in range(nt):
+        for slot in range(chips):
             pltpu.make_async_copy(
                 volt_rows.at[
-                    pl.ds(time_block(slot) * (tb * rows_t), tb * rows_t), pl.ds(c * LANES, LANES)
+                    pl.ds(chip_of(slot) * (block * rows_t), block * rows_t), pl.ds(c * LANES, LANES)
                 ],
                 volt.at[slot, c],
                 volt_sem.at[c],
             ).start()
-    for copy in small[3:]:
+    for copy in small[3:] + dft_copies:
         copy.start()
 
     row = lax.broadcasted_iota(jnp.int32, (8, LANES), 0)
@@ -197,18 +222,28 @@
         for c in range(cz):
             gains[beam, c] = use * own_gain[c]
 
-    for h in range(1, halo + 1):
-
-        @pl.when(tile < h)
-        def _():
-            inbox[h] = jnp.zeros(inbox.shape[1:], F32)
+    reach = -(-(taps - 1) // block)
+
+    def rows_of(back, k):
+        shift = (halo - k) * tb - back * block
+        low = max(0, halo * tb - (taps - 1) - shift)
+        high = min(block, (halo + 1) * tb - shift)
+        return low, max(high - low, 0), low + shift
 
     unused = halo * tb - (taps - 1)
     if unused:
-        inbox[halo, :, :, pl.ds(0, unused), :] = jnp.zeros((nz, cz, unused, LANES), F32)
+        inbox[:, :, pl.ds(0, unused), :] = jnp.zeros((nz, cz, unused, LANES), F32)
+    for back in range(1, reach + 1):
+        for k in range(pair):
+            size, start = rows_of(back, k)[1:]
+            if size:
+
+                @pl.when(jnp.logical_and(chip < back, core == k))
+                def _(size=size, start=start):
+                    inbox[:, :, pl.ds(start, size), :] = jnp.zeros((nz, cz, size, LANES), F32)
 
     with jax.named_scope("barrier"):
-        pl.semaphore_wait(barrier, count)
+        pl.semaphore_wait(barrier, few + core // max(packer, 1) * (many - few) if pair > 1 else many)
 
     if exchange:
         for c in range(cz):
@@ -256,7 +291,7 @@
         w_re[c, rows, :] = jnp.where(even, weight, pltpu.roll(weight, 1, 0))
         w_im[c, rows, :] = jnp.where(even, pltpu.roll(weight, share - 1, 0), weight)
 
-    unroll = math.gcd(tb, 8)
+    unroll = math.gcd(block, 8)
 
     def accumulate(slot, c, starts, extend):
         def step(s, carry):
@@ -279,15 +314,12 @@
                     acc[slot, c, rows, :] = acc[slot, c, rows, :] + value if extend else value
             return carry
 
-        if tb == unroll:
-            step(0, 0)
-        else:
-            lax.fori_loop(0, tb // unroll, step, 0)
+        lax.fori_loop(0, block // unroll, step, 0)
 
     def take(slot, c, which, p, ri):
         total = None
         for half in range(2):
-            value = acc[slot, c, pl.ds(which * 8 + half * 4 + p * 2 + ri, tb, stride=16), :]
+            value = acc[slot, c, pl.ds(which * 8 + half * 4 + p * 2 + ri, block, stride=16), :]
             total = value if total is None else total + value
         return total
 
@@ -304,7 +336,7 @@
                     accumulate(slot, c, starts[:1], False)
                     return carry
 
-                lax.fori_loop(0, nt, first_sum, 0)
+                lax.fori_loop(0, chips, first_sum, 0)
     for c in range(cz):
         with jax.named_scope(f"gainwait{c}"):
             if exchange:
@@ -313,7 +345,7 @@
                 wait_all(volt.at[:, c], volt_sem.at[c])
         for db in range(1, nb if exchange else 1):
             weigh(c, starts[db], gains[lax.rem(beam + db, nb), c])
-        for slot in range(nt):
+        for slot in range(chips):
             if exchange:
                 accumulate(slot, c, starts[1:], True)
             else:
@@ -321,43 +353,20 @@
             for p in range(2):
                 part[slot, c, p * 2] = take(slot, c, 0, p, 0) - take(slot, c, 1, p, 1)
                 part[slot, c, p * 2 + 1] = take(slot, c, 0, p, 1) + take(slot, c, 1, p, 0)
-            if slot < nt - 1:
+            def send(slot=slot, c=c):
                 pltpu.make_async_remote_copy(
                     src_ref=part.at[slot, c],
-                    dst_ref=recv.at[slot, c],
-                    send_sem=part_send.at[0],
+                    dst_ref=recv.at[slot * pair + core, c],
+                    send_sem=part_send.at[slot],
                     recv_sem=part_recv.at[c],
-                    device_id=peer(time_block(slot), chan, beam),
+                    device_id=peer(packer_of(chip_of(slot)), chan, beam),
                     device_id_type=MESH,
                 ).start()
 
-    for copy in small[3:]:
-        copy.wait()
-    kdim = 4 * nz * fz
-    moved = jnp.zeros((4 * tb, cz * LANES), F32)
-    for c in range(cz):
-        with jax.named_scope(f"partwait{c}"):
-            wait_all(recv.at[:, c], part_recv.at[c])
-        sums = part[nt - 1, c]
-        for slot in range(nt - 1):
-            sums = sums + recv[slot, c]
-        sums = sums.reshape(4 * tb, LANES)
-        high = sums.astype(BF16)
-        low = (sums - high.astype(F32)).astype(BF16)
-        table = table_ref[pl.ds(2 * kdim + c * LANES, LANES), pl.ds(0, cz * LANES)]
-        moved = moved + jnp.dot(high, table, preferred_element_type=F32)
-        moved = moved + jnp.dot(low, table, preferred_element_type=F32)
-    group = lax.broadcasted_iota(jnp.int32, (tb, LANES), 1) // fz
-    for z in range(nz):
-        for c in range(cz):
-            total = None
-            for g in range(4):
-                value = moved[g * tb : (g + 1) * tb, c * LANES : (c + 1) * LANES]
-                shift = (g - z) * fz % LANES
-                if shift:
-                    value = pltpu.roll(value, shift, 1)
-                total = value if g == 0 else jnp.where(group == g, value, total)
-            packed[z, c] = total
+            if slot < chips - 1:
+                send()
+            elif pair > 1:
+                pl.when(jnp.logical_not(packs))(send)
 
     half = 2 * chan // nz
     place = chan * half + (nz - 1 - chan) * (1 - half)
@@ -368,55 +377,99 @@
         other = i + (i + nz - place) // nz
         return other * half + (nz - 1 - other) * (1 - half)
 
-    def halo_rows(h):
-        count = tb if h < halo else taps - 1 - (halo - 1) * tb
-        return pl.ds(tb - count, count)
-
-    messages = [(h, i) for i in range(nz) for h in range(halo + 1) if h or i < nz - 1]
-
-    for h, i in messages:
-
-        def send(h=h, i=i):
-            pltpu.make_async_remote_copy(
-                src_ref=packed.at[target(i), :, halo_rows(h), :],
-                dst_ref=inbox.at[h, chan, :, halo_rows(h), :],
-                send_sem=pack_send.at[h],
-                recv_sem=pack_recv.at[h],
-                device_id=peer(lax.rem(tile + h, nt), target(i), beam),
-                device_id_type=MESH,
-            ).start()
-
-        if h == 0:
-            send()
-        else:
-            pl.when(tile + h < nt)(send)
-
-    inbox[0, chan] = packed[chan]
+    for copy in small[3:]:
+        copy.wait()
+
+    @pl.when(packs)
+    def _():
+        moved = jnp.zeros((4 * block, cz * LANES), F32)
+        for c in range(cz):
+            with jax.named_scope(f"partwait{c}"):
+                wait_all(recv.at[:, c], part_recv.at[c])
+            sums = part[chips - 1, c]
+            for i in range(nt - 1):
+                sums = sums + recv[i, c]
+            sums = sums.reshape(4 * block, LANES)
+            high = sums.astype(BF16)
+            low = (sums - high.astype(F32)).astype(BF16)
+            table = perm_ref[pl.ds(c * LANES, LANES), :]
+            both = jnp.dot(
+                jnp.concatenate([high, low], axis=0), table, preferred_element_type=F32
+            )
+            moved = moved + both[: 4 * block] + both[4 * block :]
+        group = lax.broadcasted_iota(jnp.int32, (block, LANES), 1) // fz
+        for c in range(cz):
+            turned = []
+            for g in range(4):
+                value = moved[g * block : (g + 1) * block, c * LANES : (c + 1) * LANES]
+                turned.append(pltpu.roll(value, g * fz, 1) if g else value)
+            for z in range(nz):
+                total = turned[0]
+                for g in range(1, 4):
+                    total = jnp.where(group == (g + z) % 4, turned[g], total)
+                packed[z, c] = total
+
+        for i in range(nz):
+            for back in range(reach + 1):
+                for k in range(pair):
+                    begin, size, start = rows_of(back, k)
+                    if not size or (i == nz - 1 and back == 0 and k == packer):
+                        continue
+
+                    def send(i=i, back=back, k=k, begin=begin, size=size, start=start):
+                        pltpu.make_async_remote_copy(
+                            src_ref=packed.at[target(i), :, pl.ds(begin, size), :],
+                            dst_ref=inbox.at[chan, :, pl.ds(start, size), :],
+                            send_sem=pack_send.at[back, k],
+                            recv_sem=pack_recv.at[back],
+                            device_id=peer(lax.rem(chip + back, chips) * pair + k, target(i), beam),
+                            device_id_type=MESH,
+                        ).start()
+
+                    if back == 0:
+                        send()
+                    else:
+                        pl.when(chip + back < chips)(send)
+
+        begin, size, start = rows_of(0, packer)
+        inbox[chan, :, pl.ds(start, size), :] = packed[chan, :, pl.ds(begin, size), :]
+
+    for copy in dft_copies:
+        copy.wait()
+
+    def each_group(sends):
+        for back in range(reach + 1):
+            for k in range(pair):
+                begin, size, start = rows_of(back, k)
+                if not size:
+                    continue
+                count = nz - 1 if back == 0 and k == packer else nz
+                there = packs if sends else core == k
+                if back:
+                    there = jnp.logical_and(there, chip + back < chips if sends else chip >= back)
+
+                @pl.when(there)
+                def _(back=back, k=k, count=count, begin=begin, size=size, start=start):
+                    if sends:
+                        wait_all(packed.at[pl.ds(0, count), :, pl.ds(begin, size), :], pack_send.at[back, k])
+                    else:
+                        wait_all(inbox.at[pl.ds(0, count), :, pl.ds(start, size), :], pack_recv.at[back])
 
     with jax.named_scope("packwait"):
-        for h in range(halo + 1):
-            if h == 0:
-                wait_all(inbox.at[0, pl.ds(0, nz - 1)], pack_recv.at[0])
-            else:
-
-                @pl.when(tile >= h)
-                def _():
-                    wait_all(inbox.at[h, :, :, halo_rows(h), :], pack_recv.at[h])
+        each_group(False)
 
     lhs = jnp.concatenate(
-        [
-            jnp.concatenate([inbox[h, z, c] for z in range(nz)], axis=1)
-            for c in range(cz)
-            for h in range(halo, -1, -1)
-        ],
-        axis=0,
+        [jnp.concatenate([inbox[z, c] for z in range(nz)], axis=1) for c in range(cz)], axis=0
     )
     high = lhs.astype(BF16)
     low = (lhs - high.astype(F32)).astype(BF16)
+    kdim = nz * 4 * fz
+    dft_h = dft_ref[:nz].reshape(kdim, 4 * nz * fz)
+    dft_l = dft_ref[nz:].reshape(kdim, 4 * nz * fz)
+    both = jnp.dot(jnp.concatenate([high, low], axis=0), dft_h, preferred_element_type=F32)
+    half_rows = lhs.shape[0]
     spec[...] = (
-        jnp.dot(high, table_ref[pl.ds(0, kdim), :], preferred_element_type=F32)
-        + jnp.dot(low, table_ref[pl.ds(0, kdim), :], preferred_element_type=F32)
-        + jnp.dot(high, table_ref[pl.ds(kdim, kdim), :], preferred_element_type=F32)
+        both[:half_rows] + both[half_rows:] + jnp.dot(high, dft_l, preferred_element_type=F32)
     )
     span = (halo + 1) * tb
     for c in range(cz):
@@ -433,15 +486,16 @@
     with jax.named_scope("sendwait"):
         if exchange:
             wait_all(gains.at[pl.ds(0, nb - 1)], gain_send.at[0])
-        wait_all(recv, part_send.at[0])
-        for h in range(halo + 1):
-            if h == 0:
-                wait_all(packed.at[pl.ds(0, nz - 1)], pack_send.at[0])
-            else:
-
-                @pl.when(tile + h < nt)
+        for slot in range(chips):
+            if slot < chips - 1:
+                wait_all(part.at[slot], part_send.at[slot])
+            elif pair > 1:
+
+                @pl.when(jnp.logical_not(packs))
                 def _():
-                    wait_all(packed.at[:, :, halo_rows(h), :], pack_send.at[h])
+                    wait_all(part.at[chips - 1], part_send.at[chips - 1])
+
+        each_group(True)
 
 
 def store(value_ref, out_ref, sem):
@@ -466,44 +520,48 @@
         gain = gain * tile_flags.astype(F32)[:, None, None, None]
         gain = lax.all_gather(gain, "beam", axis=0, tiled=True)
     perm = gather_table(nz, fz, cz)
-    perm = np.pad(perm, ((0, 0), (0, 4 * k - perm.shape[1])))
-    table = np.concatenate([*dft_table(nz, fz), perm])
+    dft = np.stack(dft_table(nz, fz)).reshape(2 * nz, 4, fz, 4 * k)
     cfg = (nt, nz, nb, tb, n_all, taps, fz, cz, halo, exchange)
     vmem = pl.BlockSpec(memory_space=pltpu.VMEM)
     anywhere = pl.BlockSpec(memory_space=pltpu.HBM)
     span = (halo + 1) * tb
     dma = pltpu.SemaphoreType.DMA
+    pair = 2 if nt % 2 == 0 else 1
+    chips = nt // pair
+    reach = -(-(taps - 1) // (pair * tb))
     out = pl.pallas_call(
         functools.partial(kernel, cfg),
         out_shape=pltpu.VMEM((tb, cz, 2, 2 * k), F32),
-        in_specs=[anywhere] * 7,
+        in_specs=[anywhere] * 8,
         out_specs=vmem,
         scratch_shapes=[
             pltpu.SMEM(tile_flags.shape, jnp.int32),
             pltpu.VMEM(delays.shape[::-1], F32),
             pltpu.SMEM(pointing.shape, jnp.int32),
             pltpu.VMEM(synth_filter.shape, F32),
-            pltpu.VMEM(table.shape, BF16),
-            pltpu.VMEM((nt, cz, tb * n_all * 4, LANES), BF16),
+            pltpu.VMEM(perm.shape, BF16),
+            pltpu.VMEM(dft.shape, BF16),
+            pltpu.VMEM((chips, cz, pair * tb * n_all * 4, LANES), BF16),
             pltpu.VMEM((cz, gain.shape[0] * 4, LANES), F32),
             pltpu.VMEM((nb, cz, n_own * 4, LANES), F32),
             pltpu.VMEM((cz, n_all * 4, LANES), F32),
             pltpu.VMEM((cz, n_all * 4, LANES), F32),
-            pltpu.VMEM((nt, cz, tb * 16, LANES), F32),
-            pltpu.VMEM((nt, cz, 4, tb, LANES), F32),
-            pltpu.VMEM((nt - 1, cz, 4, tb, LANES), F32),
-            pltpu.VMEM((nz, cz, tb, LANES), F32),
-            pltpu.VMEM((halo + 1, nz, cz, tb, LANES), F32),
+            pltpu.VMEM((chips, cz, pair * tb * 16, LANES), F32),
+            pltpu.VMEM((chips, cz, 4, pair * tb, LANES), F32),
+            pltpu.VMEM((nt - 1, cz, 4, pair * tb, LANES), F32),
+            pltpu.VMEM((nz, cz, pair * tb, LANES), F32),
+            pltpu.VMEM((nz, cz, span, LANES), F32),
             pltpu.VMEM((cz * span, 4 * k), F32),
             dma((5,)),
             dma((1,)),
             dma((cz,)),
             dma((1,)),
             dma((cz,)),
+            dma((chips,)),
+            dma((cz,)),
+            dma((reach + 1, pair)),
+            dma((reach + 1,)),
             dma((1,)),
-            dma((cz,)),
-            dma((halo + 1,)),
-            dma((halo + 1,)),
         ],
         compiler_params=pltpu.CompilerParams(collective_id=0, has_side_effects=True),
     )(
@@ -513,7 +571,8 @@
         delays.T,
         pointing,
         synth_filter,
-        jnp.asarray(table),
+        jnp.asarray(perm),
+        jnp.asarray(dft),
     )
     final = pl.pallas_call(
         store,

time: 18.4 us -> 17.7 us (0.962)
  the two profiles are of different devices: /device:TPU:0 before, /device:TPU:1 now
where the time goes in v2:
time: 17.7 us; the launch traced here: 17.5 us
  Pallas kernels  16.9 us (95%)
  between operations  0.66 us (4%)
    pallas_call x1, Pallas kernels, body(): pl.pallas_call(functools.partial(kernel, cfg), out_shape=pltpu.VMEM((tb,...  16.2 us
    pallas_call x1, Pallas kernels, body(): pl.pallas_call(store, out_shape=jax.ShapeDtypeStruct(out.shape, F32), in_...  0.63 us

profile of v2, /device:TPU:1, one launch (start us, length us, event | category | flops | bytes accessed | tf_op | source)
XLA Modules:
  0.0 17.5 jit_solution(2305195315210841650)
XLA Ops:
  0.7 16.2 %shard_map.82.value_ref = f32[8,3,2,256]{3,2,1,0:T(2,128)S(1)} custom-call(bf16[2048,2,384]{2,1,0:T(2,128)(2,1)} %bitcast.8, f32[32,2,384]{2,1,0:T(2,128)} %bitcast.9, s32[16]{0:T(128)} %flag_src.1, f32[32,64]{1,0:T(8,128)} %bitcast.10, s32[1]{0:T(128)S(6)} %copy.10.point_src, f32[12,128]{1,0:T(8,128)} %synth_src.1, ...), custom_call_target="tpu_custom_call" | custom-call | tf_op jit(solution)/shard_map/pallas_call | solution.py:532
  16.9 0.6 %shard_map.83 = f32[8,3,2,256]{3,2,1,0:T(2,128)} custom-call(f32[8,3,2,256]{3,2,1,0:T(2,128)S(1)} %shard_map.82.value_ref), custom_call_target="tpu_custom_call" | custom-call | tf_op jit(solution)/shard_map/pallas_call | solution.py:577

commit v3 on v2

v3 whole, which is shorter than its diff:
```python
import functools
import math

import jax
import jax.numpy as jnp
import numpy as np
from jax import lax
from jax.experimental import pallas as pl
from jax.experimental.pallas import tpu as pltpu
from jax.sharding import PartitionSpec as P

COARSE = 12
LANES = 128
MESH = pl.DeviceIdType.MESH
F32 = jnp.float32
BF16 = jnp.bfloat16


def even_fit(func, degree):
    series = np.polynomial.chebyshev.Chebyshev.interpolate(
        lambda u: func(np.sqrt(u)), degree, domain=[0.0, 0.25]
    )
    return [float(v) for v in series.convert(kind=np.polynomial.Polynomial).coef]


COS_COEF = even_fit(lambda r: np.cos(2 * np.pi * r), 7)
SIN_COEF = even_fit(lambda r: 2 * np.pi * np.sinc(2 * r), 7)


def horner(coef, u):
    total = jnp.full_like(u, coef[-1])
    for value in coef[-2::-1]:
        total = total * u + value
    return total


def split_bf16(table):
    high = table.astype(BF16)
    low = (table - high.astype(np.float64)).astype(BF16)
    return high, low


def dft_table(nz, fz):
    k = nz * fz
    f = np.arange(k)
    m = np.arange(k)
    angle = 2 * np.pi * (f[:, None] * m[None, :] % k) / k
    cosine, sine = np.cos(angle) / math.sqrt(k), np.sin(angle) / math.sqrt(k)
    cosine, sine = cosine.reshape(nz // 2, 2, fz, k), sine.reshape(nz // 2, 2, fz, k)
    out = np.zeros((2, nz // 2, 2, 2, fz, 2, k))
    for p in range(2):
        for odd in range(2):
            place = odd ^ p
            out[p, :, place, 0, :, 0], out[p, :, place, 0, :, 1] = cosine[:, odd], sine[:, odd]
            out[p, :, place, 1, :, 0], out[p, :, place, 1, :, 1] = -sine[:, odd], cosine[:, odd]
    return split_bf16(out.reshape(nz, 4, fz, 2 * k))


def gather_table(nz, fz, cz):
    width = fz * COARSE
    out = np.zeros((width, width), np.float64)
    for c in range(cz):
        for z in range(nz):
            for f in range(fz):
                out[f * COARSE + z * cz + c, (c * nz + z) * fz + f] = 1.0
    return out.astype(BF16)


def kernel(
    cfg,
    volt_ref,
    gain_ref,
    flag_src,
    delay_src,
    point_src,
    synth_src,
    perm_src,
    dft_src,
    out_ref,
    flag_ref,
    delay_ref,
    point_ref,
    synth_ref,
    perm_ref,
    dft_ref,
    volt,
    own_gain,
    gains,
    w_re,
    w_im,
    acc,
    part,
    recv,
    packed,
    inbox,
    spec,
    gain_send,
    gain_recv,
    part_send,
    part_recv,
    pack_send,
    pack_recv,
):
    nt, nz, nb, tb, n_all, taps, fz, cz, halo, exchange = cfg
    tile = lax.axis_index("tile")
    chan = lax.axis_index("chan")
    beam = lax.axis_index("beam")
    rows_t = n_all * 4

    def peer(t, z, b):
        return {"tile": t, "chan": z, "beam": b}

    pair = 2 if nt % 2 == 0 else 1
    chips = nt // pair
    chip, core = lax.div(tile, pair), lax.rem(tile, pair)
    packer = pair - 1
    packs = core == packer
    order = sorted(range(1, chips), key=lambda a: abs(2 * a - chips)) + [0]
    block = pair * tb

    def chip_of(slot):
        return lax.rem(chip + order[slot], chips)

    def packer_of(target_chip):
        return target_chip * pair + packer

    span = (halo + 1) * tb

    def wait_all(ref, sem):
        pltpu.make_async_copy(ref, ref, sem).wait()

    reach = -(-(taps - 1) // block)

    def rows_of(back, k):
        shift = (halo - k) * tb - back * block
        low = max(0, halo * tb - (taps - 1) - shift)
        high = min(block, (halo + 1) * tb - shift)
        return low, max(high - low, 0), low + shift

    def early(small_sem, own_sem, volt_sem, dft_sem):
        gain_rows = gain_ref.reshape(gain_ref.shape[0] * 2, gain_ref.shape[2])
        for c in range(cz):
            pltpu.make_async_copy(
                gain_rows.at[:, pl.ds(c * LANES, LANES)], own_gain.at[c], own_sem.at[0]
            ).start()
        small = [
            pltpu.make_async_copy(src, dst, small_sem.at[i])
            for i, (src, dst) in enumerate(
                [
                    (flag_src, flag_ref),
                    (point_src, point_ref),
                    (delay_src, delay_ref),
                    (synth_src, synth_ref),
                    (perm_src, perm_ref),
                ]
            )
        ]
        dft_copies = [
            pltpu.make_async_copy(
                dft_src.at[:, g], dft_ref.at[:, lax.rem(chan + g, 4)], dft_sem.at[0]
            )
            for g in range(4)
        ]
        for copy in small[:3]:
            copy.start()

        barrier = pltpu.get_barrier_semaphore()

        def greet(t, z, b):
            pl.semaphore_signal(barrier, inc=1, device_id=peer(t, z, b), device_id_type=MESH)

        for db in range(1, nb):
            greet(tile, chan, lax.rem(beam + db, nb))
        if pair > 1:

            @pl.when(packs)
            def _():
                for a in range(chips):
                    for k in range(packer):
                        greet(lax.rem(chip + a, chips) * pair + k, chan, beam)

            @pl.when(jnp.logical_not(packs))
            def _():
                for a in range(chips):
                    greet(packer_of(lax.rem(chip + a, chips)), chan, beam)

        for dz in range(nz):
            for a in range(chips):
                if dz == 0:
                    if a:
                        pl.when(packs)(
                            functools.partial(greet, packer_of(lax.rem(chip + a, chips)), chan, beam)
                        )
                else:
                    greet(packer_of(lax.rem(chip + a, chips)), lax.rem(chan + dz, nz), beam)

        few = chips * (pair - 1) // max(packer, 1) + nb - 1
        many = nt * nz - 1 + nb - 1

        volt_rows = volt_ref.reshape(volt_ref.shape[0] * 2, volt_ref.shape[2])
        for c in range(cz):
            for slot in range(chips):
                pltpu.make_async_copy(
                    volt_rows.at[
                        pl.ds(chip_of(slot) * (block * rows_t), block * rows_t), pl.ds(c * LANES, LANES)
                    ],
                    volt.at[slot, c],
                    volt_sem.at[c],
                ).start()
        for copy in small[3:] + dft_copies:
            copy.start()

        row = lax.broadcasted_iota(jnp.int32, (8, LANES), 0)
        first = row < 4
        n_own = n_all // nb
        share = n_own * 4 if exchange else rows_t
        even = lax.rem(lax.broadcasted_iota(jnp.int32, (share, LANES), 0), 2) == 0

        with jax.named_scope("ownload"):
            wait_all(own_gain, own_sem.at[0])
            small[0].wait()
        if exchange:
            use = jnp.concatenate(
                [
                    jnp.where(first, flag_ref[2 * i].astype(F32), flag_ref[2 * i + 1].astype(F32))
                    for i in range(n_own // 2)
                ],
                axis=0,
            )
            for c in range(cz):
                gains[beam, c] = use * own_gain[c]

        unused = halo * tb - (taps - 1)
        if unused:
            inbox[:, :, pl.ds(0, unused), :] = jnp.zeros((nz, cz, unused, LANES), F32)
        for back in range(1, reach + 1):
            for k in range(pair):
                size, start = rows_of(back, k)[1:]
                if size:

                    @pl.when(jnp.logical_and(chip < back, core == k))
                    def _(size=size, start=start):
                        inbox[:, :, pl.ds(start, size), :] = jnp.zeros((nz, cz, size, LANES), F32)

        with jax.named_scope("barrier"):
            pl.semaphore_wait(barrier, few + core // max(packer, 1) * (many - few) if pair > 1 else many)

        if exchange:
            for c in range(cz):
                for db in range(1, nb):
                    pltpu.make_async_remote_copy(
                        src_ref=gains.at[beam, c],
                        dst_ref=gains.at[beam, c],
                        send_sem=gain_send.at[0],
                        recv_sem=gain_recv.at[c],
                        device_id=peer(tile, chan, lax.rem(beam + db, nb)),
                        device_id_type=MESH,
                    ).start()

        for copy in small[1:3]:
            copy.wait()
        select = lax.broadcasted_iota(jnp.int32, delay_ref.shape, 1) == point_ref[0]
        delay = jnp.sum(jnp.where(select, delay_ref[...], 0.0), axis=1, keepdims=True)
        delay = jnp.broadcast_to(delay, (n_all, LANES))
        delay = jnp.concatenate(
            [
                jnp.where(
                    first,
                    jnp.broadcast_to(delay[2 * i : 2 * i + 1], (8, LANES)),
                    jnp.broadcast_to(delay[2 * i + 1 : 2 * i + 2], (8, LANES)),
                )
                for i in range(n_all // 2)
            ],
            axis=0,
        )
        for c in range(cz):
            local = (lax.broadcasted_iota(jnp.int32, (1, LANES), 1) + c * LANES).astype(F32)
            fine = jnp.floor((local + 0.5) / COARSE)
            channel = (local - COARSE * fine) * (nz * fz) + fine + (chan * fz).astype(F32)
            frequency = (channel + 0.5) / (COARSE * nz * fz)
            cycles = delay * frequency
            turn = cycles - jnp.floor(cycles + 0.5)
            square = turn * turn
            w_re[c] = horner(COS_COEF, square)
            w_im[c] = turn * horner(SIN_COEF, square)

        def weigh(c, start, gain):
            rows = pl.ds(start, share)
            swapped = jnp.where(even, pltpu.roll(gain, share - 1, 0), -pltpu.roll(gain, 1, 0))
            weight = gain * w_re[c, rows, :] + swapped * w_im[c, rows, :]
            w_re[c, rows, :] = jnp.where(even, weight, pltpu.roll(weight, 1, 0))
            w_im[c, rows, :] = jnp.where(even, pltpu.roll(weight, share - 1, 0), weight)

        unroll = math.gcd(block, 8)

        def accumulate(slot, c, starts, extend):
            def step(s, carry):
                sums = [[jnp.zeros((16, LANES), F32)] * 2 for _ in range(unroll)]
                for start in starts:
                    for q in range(share // 16):
                        at = start + q * 16
                        wr = w_re[c, pl.ds(at, 16), :]
                        wi = w_im[c, pl.ds(at, 16), :]
                        for u in range(unroll):
                            begin = pl.multiple_of((s * unroll + u) * rows_t + at, 16)
                            v = volt[slot, c, pl.ds(begin, 16), :].astype(F32)
                            sums[u] = [sums[u][0] + wr * v, sums[u][1] + wi * v]
                for u in range(unroll):
                    begin = pl.multiple_of((s * unroll + u) * 16, 16)
                    for which in range(2):
                        value = sums[u][which]
                        value = value[:8] + value[8:]
                        rows = pl.ds(begin + which * 8, 8)
                        acc[slot, c, rows, :] = acc[slot, c, rows, :] + value if extend else value
                return carry

            lax.fori_loop(0, block // unroll, step, 0)

        def take(slot, c, which, p, ri):
            total = None
            for half in range(2):
                value = acc[slot, c, pl.ds(which * 8 + half * 4 + p * 2 + ri, block, stride=16), :]
                total = value if total is None else total + value
            return total

        starts = [0]
        if exchange:
            starts = [pl.multiple_of(lax.rem(beam + db, nb) * share, 16) for db in range(nb)]
        with jax.named_scope("acc1"):
            for c in range(cz):
                weigh(c, starts[0], gains[beam, c] if exchange else own_gain[c])
                if exchange:
                    wait_all(volt.at[:, c], volt_sem.at[c])

                    def first_sum(slot, carry, c=c):
                        accumulate(slot, c, starts[:1], False)
                        return carry

                    lax.fori_loop(0, chips, first_sum, 0)
        for c in range(cz):
            with jax.named_scope(f"gainwait{c}"):
                if exchange:
                    wait_all(gains.at[pl.ds(0, nb - 1), c], gain_recv.at[c])
                else:
                    wait_all(volt.at[:, c], volt_sem.at[c])
            for db in range(1, nb if exchange else 1):
                weigh(c, starts[db], gains[lax.rem(beam + db, nb), c])
            for slot in range(chips):
                if exchange:
                    accumulate(slot, c, starts[1:], True)
                else:
                    accumulate(slot, c, starts, False)
                for p in range(2):
                    part[slot, c, p * 2] = take(slot, c, 0, p, 0) - take(slot, c, 1, p, 1)
                    part[slot, c, p * 2 + 1] = take(slot, c, 0, p, 1) + take(slot, c, 1, p, 0)
                def send(slot=slot, c=c):
                    pltpu.make_async_remote_copy(
                        src_ref=part.at[slot, c],
                        dst_ref=recv.at[slot * pair + core, c],
                        send_sem=part_send.at[slot],
                        recv_sem=part_recv.at[c],
                        device_id=peer(packer_of(chip_of(slot)), chan, beam),
                        device_id_type=MESH,
                    ).start()

                if slot < chips - 1:
                    send()
                elif pair > 1:
                    pl.when(jnp.logical_not(packs))(send)

        half = 2 * chan // nz
        place = chan * half + (nz - 1 - chan) * (1 - half)

        def target(i):
            if i == nz - 1:
                return chan
            other = i + (i + nz - place) // nz
            return other * half + (nz - 1 - other) * (1 - half)

        for copy in small[3:]:
            copy.wait()

        @pl.when(packs)
        def _():
            moved = jnp.zeros((4 * block, cz * LANES), F32)
            for c in range(cz):
                with jax.named_scope(f"partwait{c}"):
                    wait_all(recv.at[:, c], part_recv.at[c])
                sums = part[chips - 1, c]
                for i in range(nt - 1):
                    sums = sums + recv[i, c]
                sums = sums.reshape(4 * block, LANES)
                high = sums.astype(BF16)
                low = (sums - high.astype(F32)).astype(BF16)
                table = perm_ref[pl.ds(c * LANES, LANES), :]
                both = jnp.dot(
                    jnp.concatenate([high, low], axis=0), table, preferred_element_type=F32
                )
                moved = moved + both[: 4 * block] + both[4 * block :]
            group = lax.broadcasted_iota(jnp.int32, (block, LANES), 1) // fz
            quarter = 2 * lax.rem(chan, 2)
            turned = [
                [
                    pltpu.roll(
                        moved[g * block : (g + 1) * block, c * LANES : (c + 1) * LANES],
                        lax.rem(quarter + g, 4) * fz,
                        1,
                    )
                    for g in range(4)
                ]
                for c in range(cz)
            ]
            for i in range(nz):
                z = target(i)
                for c in range(cz):
                    total = turned[c][0]
                    for g in range(1, 4):
                        total = jnp.where(group == lax.rem(quarter + g + z, 4), turned[c][g], total)
                    packed[z, c] = total
            messages = sorted(
                (i + (0.5 if k == packer else 2.5) * (back > 0), i, back, k)
                for i in range(nz)
                for back in range(reach + 1)
                for k in range(pair)
                if rows_of(back, k)[1] and (i < nz - 1 or back or k < packer)
            )
            for _, i, back, k in messages:
                begin, size, start = rows_of(back, k)

                def send(i=i, back=back, k=k, begin=begin, size=size, start=start):
                    pltpu.make_async_remote_copy(
                        src_ref=packed.at[target(i), :, pl.ds(begin, size), :],
                        dst_ref=inbox.at[chan, :, pl.ds(start, size), :],
                        send_sem=pack_send.at[back, k],
                        recv_sem=pack_recv.at[back],
                        device_id=peer(lax.rem(chip + back, chips) * pair + k, target(i), beam),
                        device_id_type=MESH,
                    ).start()

                if back == 0:
                    send()
                else:
                    pl.when(chip + back < chips)(send)

            begin, size, start = rows_of(0, packer)
            inbox[chan, :, pl.ds(start, size), :] = packed[chan, :, pl.ds(begin, size), :]

        for copy in dft_copies:
            copy.wait()

    dma = pltpu.SemaphoreType.DMA
    pl.run_scoped(early, dma((5,)), dma((1,)), dma((cz,)), dma((1,)))

    def each_group(sends):
        for back in range(reach + 1):
            for k in range(pair):
                begin, size, start = rows_of(back, k)
                if not size:
                    continue
                count = nz - 1 if back == 0 and k == packer else nz
                there = packs if sends else core == k
                if back:
                    there = jnp.logical_and(there, chip + back < chips if sends else chip >= back)

                @pl.when(there)
                def _(back=back, k=k, count=count, begin=begin, size=size, start=start):
                    if sends:
                        wait_all(packed.at[pl.ds(0, count), :, pl.ds(begin, size), :], pack_send.at[back, k])
                    else:
                        wait_all(inbox.at[pl.ds(0, count), :, pl.ds(start, size), :], pack_recv.at[back])

    with jax.named_scope("packwait"):
        each_group(False)

    lane = lax.broadcasted_iota(jnp.int32, (span, LANES), 1) // fz
    early_half = lax.rem(lane + 4 - lax.rem(chan, 4), 4) < 2
    for p in range(2):
        lhs = jnp.concatenate(
            [
                jnp.concatenate(
                    [
                        jnp.where(early_half, inbox[2 * j + p, c], inbox[2 * j + 1 - p, c])
                        for j in range(nz // 2)
                    ],
                    axis=1,
                )
                for c in range(cz)
            ],
            axis=0,
        )
        high = lhs.astype(BF16)
        low = (lhs - high.astype(F32)).astype(BF16)
        dft_h, dft_l = [
            dft_ref[pl.ds(at + p * (nz // 2), nz // 2)].reshape(nz // 2 * 4 * fz, 2 * nz * fz)
            for at in (0, nz)
        ]
        both = jnp.dot(jnp.concatenate([high, low], axis=0), dft_h, preferred_element_type=F32)
        spec[p] = (
            both[: cz * span]
            + both[cz * span :]
            + jnp.dot(high, dft_l, preferred_element_type=F32)
        )
    for c in range(cz):
        for g in range(4):
            total = None
            for k in range(taps):
                value = synth_ref[pl.ds(k, 1), :] * spec[
                    g // 2, pl.ds(c * span + halo * tb - k, tb), g % 2 * LANES : (g % 2 + 1) * LANES
                ]
                total = value if total is None else total + value
            for t in range(tb):
                out_ref[t, c, pl.ds(g // 2, 1), (g % 2) * LANES : (g % 2 + 1) * LANES] = total[t : t + 1]

    with jax.named_scope("sendwait"):
        if exchange:
            wait_all(gains.at[pl.ds(0, nb - 1)], gain_send.at[0])
        for slot in range(chips):
            if slot < chips - 1:
                wait_all(part.at[slot], part_send.at[slot])
            elif pair > 1:

                @pl.when(jnp.logical_not(packs))
                def _():
                    wait_all(part.at[chips - 1], part_send.at[chips - 1])

        each_group(True)


def store(value_ref, out_ref, sem):
    copy = pltpu.make_async_copy(value_ref, out_ref, sem)
    copy.start()
    copy.wait()


def body(mesh, voltages, calib_gain, tile_flags, delays, pointing, synth_filter):
    nt, nz, nb = mesh.shape["tile"], mesh.shape["chan"], mesh.shape["beam"]
    total_rows, n_all = voltages.shape[:2]
    width = voltages.shape[-1]
    taps, k = synth_filter.shape
    tb = total_rows // nt
    fz = width // COARSE
    cz = COARSE // nz
    halo = -(-(taps - 1) // tb)
    n_own = calib_gain.shape[0]
    exchange = n_own % 4 == 0 and mesh.shape["beam"] > 1
    gain = calib_gain
    if not exchange:
        gain = gain * tile_flags.astype(F32)[:, None, None, None]
        gain = lax.all_gather(gain, "beam", axis=0, tiled=True)
    perm = gather_table(nz, fz, cz)
    dft = np.concatenate(dft_table(nz, fz))
    cfg = (nt, nz, nb, tb, n_all, taps, fz, cz, halo, exchange)
    vmem = pl.BlockSpec(memory_space=pltpu.VMEM)
    anywhere = pl.BlockSpec(memory_space=pltpu.HBM)
    span = (halo + 1) * tb
    dma = pltpu.SemaphoreType.DMA
    pair = 2 if nt % 2 == 0 else 1
    chips = nt // pair
    reach = -(-(taps - 1) // (pair * tb))
    out = pl.pallas_call(
        functools.partial(kernel, cfg),
        out_shape=pltpu.VMEM((tb, cz, 2, 2 * k), F32),
        in_specs=[anywhere] * 8,
        out_specs=vmem,
        scratch_shapes=[
            pltpu.SMEM(tile_flags.shape, jnp.int32),
            pltpu.VMEM(delays.shape[::-1], F32),
            pltpu.SMEM(pointing.shape, jnp.int32),
            pltpu.VMEM(synth_filter.shape, F32),
            pltpu.VMEM(perm.shape, BF16),
            pltpu.VMEM(dft.shape, BF16),
            pltpu.VMEM((chips, cz, pair * tb * n_all * 4, LANES), BF16),
            pltpu.VMEM((cz, gain.shape[0] * 4, LANES), F32),
            pltpu.VMEM((nb, cz, n_own * 4, LANES), F32),
            pltpu.VMEM((cz, n_all * 4, LANES), F32),
            pltpu.VMEM((cz, n_all * 4, LANES), F32),
            pltpu.VMEM((chips, cz, pair * tb * 16, LANES), F32),
            pltpu.VMEM((chips, cz, 4, pair * tb, LANES), F32),
            pltpu.VMEM((nt - 1, cz, 4, pair * tb, LANES), F32),
            pltpu.VMEM((nz, cz, pair * tb, LANES), F32),
            pltpu.VMEM((nz, cz, span, LANES), F32),
            pltpu.VMEM((2, cz * span, 2 * k), F32),
            dma((1,)),
            dma((cz,)),
            dma((chips,)),
            dma((cz,)),
            dma((reach + 1, pair)),
            dma((reach + 1,)),
        ],
        compiler_params=pltpu.CompilerParams(collective_id=0, has_side_effects=True),
    )(
        voltages.reshape(-1, 2, width),
        gain.reshape(-1, 2, width),
        tile_flags,
        delays.T,
        pointing,
        synth_filter,
        jnp.asarray(perm),
        jnp.asarray(dft),
    )
    final = pl.pallas_call(
        store,
        out_shape=jax.ShapeDtypeStruct(out.shape, F32),
        in_specs=[vmem],
        out_specs=pl.BlockSpec(memory_space=pltpu.HBM),
        scratch_shapes=[dma(())],
    )(pltpu.with_memory_space_constraint(out, pltpu.VMEM))
    return final.transpose(0, 2, 1, 3)[:, None]


def solution(mesh):
    in_specs = (
        P(None, "tile", None, None, "chan"),
        P(("tile", "beam"), None, None, "chan"),
        P(("tile", "beam")),
        P(None, "tile"),
        P("beam"),
        P(),
    )
    out_specs = P("tile", "beam", None, "chan", None)
    return jax.shard_map(
        functools.partial(body, mesh), mesh=mesh, in_specs=in_specs, out_specs=out_specs, check_vma=False
    )
```

time: 17.7 us -> 17.3 us (0.977)
  the two profiles are of different devices: /device:TPU:1 before, /device:TPU:2 now
where the time goes in v3:
time: 17.3 us; the launch traced here: 17.2 us
  Pallas kernels  16.5 us (95%)
  between operations  0.66 us (4%)
    pallas_call x1, Pallas kernels, body(): pl.pallas_call(functools.partial(kernel, cfg), out_shape=pltpu.VMEM((tb,...  15.9 us
    pallas_call x1, Pallas kernels, body(): pl.pallas_call(store, out_shape=jax.ShapeDtypeStruct(out.shape, F32), in_...  0.63 us

profile of v3, /device:TPU:2, one launch (start us, length us, event | category | flops | bytes accessed | tf_op | source)
XLA Modules:
  0.0 17.2 jit_solution(1284108400650185163)
XLA Ops:
  0.7 15.9 %shard_map.82.value_ref = f32[8,3,2,256]{3,2,1,0:T(2,128)S(1)} custom-call(bf16[2048,2,384]{2,1,0:T(2,128)(2,1)} %bitcast.8, f32[32,2,384]{2,1,0:T(2,128)} %bitcast.9, s32[16]{0:T(128)} %flag_src.1, f32[32,64]{1,0:T(8,128)} %bitcast.10, s32[1]{0:T(128)S(6)} %copy.10.point_src, f32[12,128]{1,0:T(8,128)} %synth_src.1, ...), custom_call_target="tpu_custom_call" | custom-call | tf_op jit(solution)/shard_map/pallas_call | solution.py:560
  16.6 0.6 %shard_map.83 = f32[8,3,2,256]{3,2,1,0:T(2,128)} custom-call(f32[8,3,2,256]{3,2,1,0:T(2,128)S(1)} %shard_map.82.value_ref), custom_call_target="tpu_custom_call" | custom-call | tf_op jit(solution)/shard_map/pallas_call | solution.py:601

commit v4 on v3

--- a/solution.py
+++ b/solution.py
@@ -100,6 +100,7 @@
     part_recv,
     pack_send,
     pack_recv,
+    ready,
 ):
     nt, nz, nb, tb, n_all, taps, fz, cz, halo, exchange = cfg
     tile = lax.axis_index("tile")
@@ -170,7 +171,9 @@
             pl.semaphore_signal(barrier, inc=1, device_id=peer(t, z, b), device_id_type=MESH)
 
         for db in range(1, nb):
-            greet(tile, chan, lax.rem(beam + db, nb))
+            greet(chip * pair, chan, lax.rem(beam + db, nb))
+            if pair > 1:
+                pl.when(packs)(functools.partial(greet, tile, chan, lax.rem(beam + db, nb)))
         if pair > 1:
 
             @pl.when(packs)
@@ -193,9 +196,6 @@
                         )
                 else:
                     greet(packer_of(lax.rem(chip + a, chips)), lax.rem(chan + dz, nz), beam)
-
-        few = chips * (pair - 1) // max(packer, 1) + nb - 1
-        many = nt * nz - 1 + nb - 1
 
         volt_rows = volt_ref.reshape(volt_ref.shape[0] * 2, volt_ref.shape[2])
         for c in range(cz):
@@ -243,7 +243,28 @@
                         inbox[:, :, pl.ds(start, size), :] = jnp.zeros((nz, cz, size, LANES), F32)
 
         with jax.named_scope("barrier"):
-            pl.semaphore_wait(barrier, few + core // max(packer, 1) * (many - few) if pair > 1 else many)
+            if pair > 1:
+
+                @pl.when(jnp.logical_not(packs))
+                def _():
+                    pl.semaphore_wait(barrier, chips + (nb - 1) * pair)
+                    pl.semaphore_signal(
+                        ready,
+                        inc=1,
+                        device_id=peer(packer_of(chip), chan, beam),
+                        device_id_type=MESH,
+                    )
+
+                @pl.when(jnp.logical_and(packs, chan < nz - 1))
+                def _():
+                    pl.semaphore_wait(ready, 1)
+
+                @pl.when(jnp.logical_and(packs, chan == nz - 1))
+                def _():
+                    pl.semaphore_wait(barrier, nt * nz - 1 + nb - 1)
+
+            else:
+                pl.semaphore_wait(barrier, nt * nz - 1 + nb - 1)
 
         if exchange:
             for c in range(cz):
@@ -337,6 +358,17 @@
                         return carry
 
                     lax.fori_loop(0, chips, first_sum, 0)
+        if pair > 1:
+
+            @pl.when(jnp.logical_and(packs, chan < nz - 1))
+            def _():
+                with jax.named_scope("barrier2"):
+                    pl.semaphore_wait(barrier, nt * nz - 1 + nb - 1)
+
+            @pl.when(jnp.logical_and(packs, chan == nz - 1))
+            def _():
+                pl.semaphore_wait(ready, 1)
+
         for c in range(cz):
             with jax.named_scope(f"gainwait{c}"):
                 if exchange:
@@ -418,7 +450,7 @@
                         total = jnp.where(group == lax.rem(quarter + g + z, 4), turned[c][g], total)
                     packed[z, c] = total
             messages = sorted(
-                (i + (0.5 if k == packer else 2.5) * (back > 0), i, back, k)
+                (i + (0.5 if k == packer else 0.6) * (back > 0), i, back, k)
                 for i in range(nz)
                 for back in range(reach + 1)
                 for k in range(pair)
@@ -586,6 +618,7 @@
             dma((cz,)),
             dma((reach + 1, pair)),
             dma((reach + 1,)),
+            pltpu.SemaphoreType.REGULAR,
         ],
         compiler_params=pltpu.CompilerParams(collective_id=0, has_side_effects=True),
     )(

time: 17.3 us -> 16.9 us (0.977)
  the two profiles are of different devices: /device:TPU:2 before, /device:TPU:0 now
where the time goes in v4:
time: 16.9 us; the launch traced here: 16.8 us
  Pallas kernels  16.1 us (95%)
  between operations  0.66 us (4%)
    pallas_call x1, Pallas kernels, body(): pl.pallas_call(functools.partial(kernel, cfg), out_shape=pltpu.VMEM((tb,...  15.5 us
    pallas_call x1, Pallas kernels, body(): pl.pallas_call(store, out_shape=jax.ShapeDtypeStruct(out.shape, F32), in_...  0.63 us

profile of v4, /device:TPU:0, one launch (start us, length us, event | category | flops | bytes accessed | tf_op | source)
XLA Modules:
  0.0 16.8 jit_solution(6719245913206865851)
XLA Ops:
  0.7 15.5 %shard_map.82.value_ref = f32[8,3,2,256]{3,2,1,0:T(2,128)S(1)} custom-call(bf16[2048,2,384]{2,1,0:T(2,128)(2,1)} %bitcast.8, f32[32,2,384]{2,1,0:T(2,128)} %bitcast.9, s32[16]{0:T(128)} %flag_src.1, f32[32,64]{1,0:T(8,128)} %bitcast.10, s32[1]{0:T(128)S(6)} %copy.10.point_src, f32[12,128]{1,0:T(8,128)} %synth_src.1, ...), custom_call_target="tpu_custom_call" | custom-call | tf_op jit(solution)/shard_map/pallas_call | solution.py:592
  16.1 0.6 %shard_map.83 = f32[8,3,2,256]{3,2,1,0:T(2,128)} custom-call(f32[8,3,2,256]{3,2,1,0:T(2,128)S(1)} %shard_map.82.value_ref), custom_call_target="tpu_custom_call" | custom-call | tf_op jit(solution)/shard_map/pallas_call | solution.py:634

commit v5 on v4

--- a/solution.py
+++ b/solution.py
@@ -94,11 +94,9 @@
     packed,
     inbox,
     spec,
-    gain_send,
+    send_sem,
     gain_recv,
-    part_send,
     part_recv,
-    pack_send,
     pack_recv,
     ready,
 ):
@@ -131,6 +129,8 @@
         pltpu.make_async_copy(ref, ref, sem).wait()
 
     reach = -(-(taps - 1) // block)
+    n_own = n_all // nb
+    share = n_own * 4 if exchange else rows_t
 
     def rows_of(back, k):
         shift = (halo - k) * tb - back * block
@@ -212,8 +212,6 @@
 
         row = lax.broadcasted_iota(jnp.int32, (8, LANES), 0)
         first = row < 4
-        n_own = n_all // nb
-        share = n_own * 4 if exchange else rows_t
         even = lax.rem(lax.broadcasted_iota(jnp.int32, (share, LANES), 0), 2) == 0
 
         with jax.named_scope("ownload"):
@@ -272,7 +270,7 @@
                     pltpu.make_async_remote_copy(
                         src_ref=gains.at[beam, c],
                         dst_ref=gains.at[beam, c],
-                        send_sem=gain_send.at[0],
+                        send_sem=send_sem.at[0],
                         recv_sem=gain_recv.at[c],
                         device_id=peer(tile, chan, lax.rem(beam + db, nb)),
                         device_id_type=MESH,
@@ -389,7 +387,7 @@
                     pltpu.make_async_remote_copy(
                         src_ref=part.at[slot, c],
                         dst_ref=recv.at[slot * pair + core, c],
-                        send_sem=part_send.at[slot],
+                        send_sem=send_sem.at[0],
                         recv_sem=part_recv.at[c],
                         device_id=peer(packer_of(chip_of(slot)), chan, beam),
                         device_id_type=MESH,
@@ -449,30 +447,26 @@
                     for g in range(1, 4):
                         total = jnp.where(group == lax.rem(quarter + g + z, 4), turned[c][g], total)
                     packed[z, c] = total
-            messages = sorted(
-                (i + (0.5 if k == packer else 0.6) * (back > 0), i, back, k)
-                for i in range(nz)
-                for back in range(reach + 1)
-                for k in range(pair)
-                if rows_of(back, k)[1] and (i < nz - 1 or back or k < packer)
-            )
-            for _, i, back, k in messages:
-                begin, size, start = rows_of(back, k)
-
-                def send(i=i, back=back, k=k, begin=begin, size=size, start=start):
-                    pltpu.make_async_remote_copy(
-                        src_ref=packed.at[target(i), :, pl.ds(begin, size), :],
-                        dst_ref=inbox.at[chan, :, pl.ds(start, size), :],
-                        send_sem=pack_send.at[back, k],
-                        recv_sem=pack_recv.at[back],
-                        device_id=peer(lax.rem(chip + back, chips) * pair + k, target(i), beam),
-                        device_id_type=MESH,
-                    ).start()
-
-                if back == 0:
-                    send()
-                else:
-                    pl.when(chip + back < chips)(send)
+                for back in range(reach + 1):
+                    for k in range(pair) if back == 0 else range(pair - 1, -1, -1):
+                        begin, size, start = rows_of(back, k)
+                        if not size or (i == nz - 1 and back == 0 and k == packer):
+                            continue
+
+                        def send(i=i, back=back, k=k, begin=begin, size=size, start=start):
+                            pltpu.make_async_remote_copy(
+                                src_ref=packed.at[target(i), :, pl.ds(begin, size), :],
+                                dst_ref=inbox.at[chan, :, pl.ds(start, size), :],
+                                send_sem=send_sem.at[0],
+                                recv_sem=pack_recv.at[back],
+                                device_id=peer(lax.rem(chip + back, chips) * pair + k, target(i), beam),
+                                device_id_type=MESH,
+                            ).start()
+
+                        if back == 0:
+                            send()
+                        else:
+                            pl.when(chip + back < chips)(send)
 
             begin, size, start = rows_of(0, packer)
             inbox[chan, :, pl.ds(start, size), :] = packed[chan, :, pl.ds(begin, size), :]
@@ -483,26 +477,31 @@
     dma = pltpu.SemaphoreType.DMA
     pl.run_scoped(early, dma((5,)), dma((1,)), dma((cz,)), dma((1,)))
 
-    def each_group(sends):
+    def sent_rows(packing, reached):
+        rows = (nb - 1) * cz * share if exchange else 0
+        rows += (chips - packing) * cz * 4 * block
+        if packing:
+            for back in range(reached + 1):
+                for k in range(pair):
+                    count = nz - 1 if back == 0 and k == packer else nz
+                    rows += count * cz * rows_of(back, k)[1]
+        return rows
+
+    def wait_sent(packing, reached):
+        flat = acc.reshape(chips * cz * block * 16, LANES)
+        wait_all(flat.at[pl.ds(0, sent_rows(packing, reached)), :], send_sem.at[0])
+
+    with jax.named_scope("packwait"):
         for back in range(reach + 1):
             for k in range(pair):
-                begin, size, start = rows_of(back, k)
+                size, start = rows_of(back, k)[1:]
                 if not size:
                     continue
                 count = nz - 1 if back == 0 and k == packer else nz
-                there = packs if sends else core == k
-                if back:
-                    there = jnp.logical_and(there, chip + back < chips if sends else chip >= back)
-
-                @pl.when(there)
-                def _(back=back, k=k, count=count, begin=begin, size=size, start=start):
-                    if sends:
-                        wait_all(packed.at[pl.ds(0, count), :, pl.ds(begin, size), :], pack_send.at[back, k])
-                    else:
-                        wait_all(inbox.at[pl.ds(0, count), :, pl.ds(start, size), :], pack_recv.at[back])
-
-    with jax.named_scope("packwait"):
-        each_group(False)
+
+                @pl.when(jnp.logical_and(core == k, chip >= back))
+                def _(back=back, count=count, size=size, start=start):
+                    wait_all(inbox.at[pl.ds(0, count), :, pl.ds(start, size), :], pack_recv.at[back])
 
     lane = lax.broadcasted_iota(jnp.int32, (span, LANES), 1) // fz
     early_half = lax.rem(lane + 4 - lax.rem(chan, 4), 4) < 2
@@ -527,35 +526,31 @@
             for at in (0, nz)
         ]
         both = jnp.dot(jnp.concatenate([high, low], axis=0), dft_h, preferred_element_type=F32)
-        spec[p] = (
+        value = (
             both[: cz * span]
             + both[cz * span :]
             + jnp.dot(high, dft_l, preferred_element_type=F32)
         )
+        for ri in range(2):
+            spec[p * 2 + ri] = value[:, ri * LANES : (ri + 1) * LANES]
     for c in range(cz):
         for g in range(4):
             total = None
             for k in range(taps):
                 value = synth_ref[pl.ds(k, 1), :] * spec[
-                    g // 2, pl.ds(c * span + halo * tb - k, tb), g % 2 * LANES : (g % 2 + 1) * LANES
+                    g, pl.ds(c * span + halo * tb - k, tb), :
                 ]
                 total = value if total is None else total + value
             for t in range(tb):
                 out_ref[t, c, pl.ds(g // 2, 1), (g % 2) * LANES : (g % 2 + 1) * LANES] = total[t : t + 1]
 
     with jax.named_scope("sendwait"):
-        if exchange:
-            wait_all(gains.at[pl.ds(0, nb - 1)], gain_send.at[0])
-        for slot in range(chips):
-            if slot < chips - 1:
-                wait_all(part.at[slot], part_send.at[slot])
-            elif pair > 1:
-
-                @pl.when(jnp.logical_not(packs))
-                def _():
-                    wait_all(part.at[chips - 1], part_send.at[chips - 1])
-
-        each_group(True)
+        if pair > 1:
+            pl.when(jnp.logical_not(packs))(functools.partial(wait_sent, 0, 0))
+        for reached in range(min(reach, chips - 1) + 1):
+            above = chips - 1 - chip
+            here = above >= reach if reached == reach else above == reached
+            pl.when(jnp.logical_and(packs, here))(functools.partial(wait_sent, 1, reached))
 
 
 def store(value_ref, out_ref, sem):
@@ -611,12 +606,10 @@
             pltpu.VMEM((nt - 1, cz, 4, pair * tb, LANES), F32),
             pltpu.VMEM((nz, cz, pair * tb, LANES), F32),
             pltpu.VMEM((nz, cz, span, LANES), F32),
-            pltpu.VMEM((2, cz * span, 2 * k), F32),
+            pltpu.VMEM((4, cz * span, k), F32),
             dma((1,)),
             dma((cz,)),
-            dma((chips,)),
             dma((cz,)),
-            dma((reach + 1, pair)),
             dma((reach + 1,)),
             pltpu.SemaphoreType.REGULAR,
         ],

time: 16.9 us -> 16.8 us (level)
  no operation moved by 1% of the time
where the time goes in v5:
time: 16.8 us; the launch traced here: 16.6 us
  Pallas kernels  16 us (95%)
  between operations  0.66 us (4%)
    pallas_call x1, Pallas kernels, body(): pl.pallas_call(functools.partial(kernel, cfg), out_shape=pltpu.VMEM((tb,...  15.3 us
    pallas_call x1, Pallas kernels, body(): pl.pallas_call(store, out_shape=jax.ShapeDtypeStruct(out.shape, F32), in_...  0.63 us

profile of v5, /device:TPU:0, one launch (start us, length us, event | category | flops | bytes accessed | tf_op | source)
XLA Modules:
  0.0 16.6 jit_solution(14491997785765406055)
XLA Ops:
  0.7 15.3 %shard_map.82.value_ref = f32[8,3,2,256]{3,2,1,0:T(2,128)S(1)} custom-call(bf16[2048,2,384]{2,1,0:T(2,128)(2,1)} %bitcast.8, f32[32,2,384]{2,1,0:T(2,128)} %bitcast.9, s32[16]{0:T(128)} %flag_src.1, f32[32,64]{1,0:T(8,128)} %bitcast.10, s32[1]{0:T(128)S(6)} %copy.10.point_src, f32[12,128]{1,0:T(8,128)} %synth_src.1, ...), custom_call_target="tpu_custom_call" | custom-call | tf_op jit(solution)/shard_map/pallas_call | solution.py:587
  16.0 0.6 %shard_map.83 = f32[8,3,2,256]{3,2,1,0:T(2,128)} custom-call(f32[8,3,2,256]{3,2,1,0:T(2,128)S(1)} %shard_map.82.value_ref), custom_call_target="tpu_custom_call" | custom-call | tf_op jit(solution)/shard_map/pallas_call | solution.py:627

commit v6 on v5

--- a/solution.py
+++ b/solution.py
@@ -312,7 +312,7 @@
 
         unroll = math.gcd(block, 8)
 
-        def accumulate(slot, c, starts, extend):
+        def accumulate(slot, c, starts, extend, piece=None):
             def step(s, carry):
                 sums = [[jnp.zeros((16, LANES), F32)] * 2 for _ in range(unroll)]
                 for start in starts:
@@ -333,12 +333,16 @@
                         acc[slot, c, rows, :] = acc[slot, c, rows, :] + value if extend else value
                 return carry
 
-            lax.fori_loop(0, block // unroll, step, 0)
-
-        def take(slot, c, which, p, ri):
+            if piece is None:
+                lax.fori_loop(0, block // unroll, step, 0)
+            else:
+                step(piece, 0)
+
+        def take(slot, c, piece, which, p, ri):
             total = None
             for half in range(2):
-                value = acc[slot, c, pl.ds(which * 8 + half * 4 + p * 2 + ri, block, stride=16), :]
+                at = piece * unroll * 16 + which * 8 + half * 4 + p * 2 + ri
+                value = acc[slot, c, pl.ds(at, unroll, stride=16), :]
                 total = value if total is None else total + value
             return total
 
@@ -376,27 +380,31 @@
             for db in range(1, nb if exchange else 1):
                 weigh(c, starts[db], gains[lax.rem(beam + db, nb), c])
             for slot in range(chips):
-                if exchange:
-                    accumulate(slot, c, starts[1:], True)
-                else:
-                    accumulate(slot, c, starts, False)
-                for p in range(2):
-                    part[slot, c, p * 2] = take(slot, c, 0, p, 0) - take(slot, c, 1, p, 1)
-                    part[slot, c, p * 2 + 1] = take(slot, c, 0, p, 1) + take(slot, c, 1, p, 0)
-                def send(slot=slot, c=c):
-                    pltpu.make_async_remote_copy(
-                        src_ref=part.at[slot, c],
-                        dst_ref=recv.at[slot * pair + core, c],
-                        send_sem=send_sem.at[0],
-                        recv_sem=part_recv.at[c],
-                        device_id=peer(packer_of(chip_of(slot)), chan, beam),
-                        device_id_type=MESH,
-                    ).start()
-
-                if slot < chips - 1:
-                    send()
-                elif pair > 1:
-                    pl.when(jnp.logical_not(packs))(send)
+                for piece in range(block // unroll):
+                    rows = pl.ds(piece * unroll, unroll)
+                    if exchange:
+                        accumulate(slot, c, starts[1:], True, piece)
+                    else:
+                        accumulate(slot, c, starts, False, piece)
+                    for p in range(2):
+                        get = functools.partial(take, slot, c, piece)
+                        part[slot, c, p * 2, rows] = get(0, p, 0) - get(1, p, 1)
+                        part[slot, c, p * 2 + 1, rows] = get(0, p, 1) + get(1, p, 0)
+
+                    def send(slot=slot, c=c, rows=rows):
+                        pltpu.make_async_remote_copy(
+                            src_ref=part.at[slot, c, :, rows],
+                            dst_ref=recv.at[slot * pair + core, c, :, rows],
+                            send_sem=send_sem.at[0],
+                            recv_sem=part_recv.at[c],
+                            device_id=peer(packer_of(chip_of(slot)), chan, beam),
+                            device_id_type=MESH,
+                        ).start()
+
+                    if slot < chips - 1:
+                        send()
+                    elif pair > 1:
+                        pl.when(jnp.logical_not(packs))(send)
 
         half = 2 * chan // nz
         place = chan * half + (nz - 1 - chan) * (1 - half)

time: 16.8 us -> 16.7 us (level)
  no operation moved by 1% of the time
where the time goes in v6:
time: 16.7 us; the launch traced here: 16.6 us
  Pallas kernels  15.9 us (95%)
  between operations  0.66 us (4%)
    pallas_call x1, Pallas kernels, body(): pl.pallas_call(functools.partial(kernel, cfg), out_shape=pltpu.VMEM((tb,...  15.3 us
    pallas_call x1, Pallas kernels, body(): pl.pallas_call(store, out_shape=jax.ShapeDtypeStruct(out.shape, F32), in_...  0.63 us

profile of v6, /device:TPU:0, one launch (start us, length us, event | category | flops | bytes accessed | tf_op | source)
XLA Modules:
  0.0 16.6 jit_solution(748823877659484961)
XLA Ops:
  0.7 15.3 %shard_map.82.value_ref = f32[8,3,2,256]{3,2,1,0:T(2,128)S(1)} custom-call(bf16[2048,2,384]{2,1,0:T(2,128)(2,1)} %bitcast.8, f32[32,2,384]{2,1,0:T(2,128)} %bitcast.9, s32[16]{0:T(128)} %flag_src.1, f32[32,64]{1,0:T(8,128)} %bitcast.10, s32[1]{0:T(128)S(6)} %copy.10.point_src, f32[12,128]{1,0:T(8,128)} %synth_src.1, ...), custom_call_target="tpu_custom_call" | custom-call | tf_op jit(solution)/shard_map/pallas_call | solution.py:595
  15.9 0.6 %shard_map.83 = f32[8,3,2,256]{3,2,1,0:T(2,128)} custom-call(f32[8,3,2,256]{3,2,1,0:T(2,128)S(1)} %shard_map.82.value_ref), custom_call_target="tpu_custom_call" | custom-call | tf_op jit(solution)/shard_map/pallas_call | solution.py:635

commit v7 on v6

--- a/solution.py
+++ b/solution.py
@@ -228,18 +228,6 @@
             for c in range(cz):
                 gains[beam, c] = use * own_gain[c]
 
-        unused = halo * tb - (taps - 1)
-        if unused:
-            inbox[:, :, pl.ds(0, unused), :] = jnp.zeros((nz, cz, unused, LANES), F32)
-        for back in range(1, reach + 1):
-            for k in range(pair):
-                size, start = rows_of(back, k)[1:]
-                if size:
-
-                    @pl.when(jnp.logical_and(chip < back, core == k))
-                    def _(size=size, start=start):
-                        inbox[:, :, pl.ds(start, size), :] = jnp.zeros((nz, cz, size, LANES), F32)
-
         with jax.named_scope("barrier"):
             if pair > 1:
 
@@ -275,6 +263,18 @@
                         device_id=peer(tile, chan, lax.rem(beam + db, nb)),
                         device_id_type=MESH,
                     ).start()
+
+        unused = halo * tb - (taps - 1)
+        if unused:
+            inbox[:, :, pl.ds(0, unused), :] = jnp.zeros((nz, cz, unused, LANES), F32)
+        for back in range(1, reach + 1):
+            for k in range(pair):
+                size, start = rows_of(back, k)[1:]
+                if size:
+
+                    @pl.when(jnp.logical_and(chip < back, core == k))
+                    def _(size=size, start=start):
+                        inbox[:, :, pl.ds(start, size), :] = jnp.zeros((nz, cz, size, LANES), F32)
 
         for copy in small[1:3]:
             copy.wait()

time: 16.7 us -> 16.7 us (level)
  no operation moved by 1% of the time
where the time goes in v7:
time: 16.7 us; the launch traced here: 16.6 us
  Pallas kernels  15.9 us (95%)
  between operations  0.66 us (4%)
    pallas_call x1, Pallas kernels, body(): pl.pallas_call(functools.partial(kernel, cfg), out_shape=pltpu.VMEM((tb,...  15.3 us
    pallas_call x1, Pallas kernels, body(): pl.pallas_call(store, out_shape=jax.ShapeDtypeStruct(out.shape, F32), in_...  0.63 us

profile of v7, /device:TPU:0, one launch (start us, length us, event | category | flops | bytes accessed | tf_op | source)
XLA Modules:
  0.0 16.6 jit_solution(1779760785396245128)
XLA Ops:
  0.7 15.3 %shard_map.82.value_ref = f32[8,3,2,256]{3,2,1,0:T(2,128)S(1)} custom-call(bf16[2048,2,384]{2,1,0:T(2,128)(2,1)} %bitcast.8, f32[32,2,384]{2,1,0:T(2,128)} %bitcast.9, s32[16]{0:T(128)} %flag_src.1, f32[32,64]{1,0:T(8,128)} %bitcast.10, s32[1]{0:T(128)S(6)} %copy.10.point_src, f32[12,128]{1,0:T(8,128)} %synth_src.1, ...), custom_call_target="tpu_custom_call" | custom-call | tf_op jit(solution)/shard_map/pallas_call | solution.py:595
  15.9 0.6 %shard_map.83 = f32[8,3,2,256]{3,2,1,0:T(2,128)} custom-call(f32[8,3,2,256]{3,2,1,0:T(2,128)S(1)} %shard_map.82.value_ref), custom_call_target="tpu_custom_call" | custom-call | tf_op jit(solution)/shard_map/pallas_call | solution.py:635
